TPU v7x, 8 devices: a whole 2x2x1 slice. The times are simulated.
8 devices in a mesh: dp: 8 (over z, y, x, core).
Axes of the slice: x: 2, y: 2, z: 1, core: 2. Of those that a mesh axis runs over, the one named last changes fastest.
Arguments:
- grad_wq: bfloat16 [8, 2, 896, 896], P('dp')
- grad_wk: bfloat16 [8, 2, 896, 128], P('dp')
- grad_wv: bfloat16 [8, 2, 896, 128], P('dp')
- grad_wo: bfloat16 [8, 2, 896, 896], P('dp')
- grad_gate: bfloat16 [8, 2, 896, 4864], P('dp')
- grad_up: bfloat16 [8, 2, 896, 4864], P('dp')
- grad_down: bfloat16 [8, 2, 4864, 896], P('dp')
- grad_attn_norm: bfloat16 [8, 2, 896], P('dp')
- grad_mlp_norm: bfloat16 [8, 2, 896], P('dp')
- grad_final_norm: bfloat16 [8, 896], P('dp')
- master: float32 [29824000], P('dp')
- exp_avg: float32 [29824000], P('dp')
- exp_avg_sq: float32 [29824000], P('dp')
- learn_rate: float32 [], replicated
Outputs:
- output 1: float32 [29824000], P('dp')
- output 2: float32 [29824000], P('dp')
- output 3: float32 [29824000], P('dp')
- output 4: bfloat16 [2, 896, 896], replicated
- output 5: bfloat16 [2, 896, 128], replicated
- output 6: bfloat16 [2, 896, 128], replicated
- output 7: bfloat16 [2, 896, 896], replicated
- output 8: bfloat16 [2, 896, 4864], replicated
- output 9: bfloat16 [2, 896, 4864], replicated
- output 10: bfloat16 [2, 4864, 896], replicated
- output 11: bfloat16 [2, 896], replicated
- output 12: bfloat16 [2, 896], replicated
- output 13: bfloat16 [896], replicated
- output 14: float32 [], replicated
All inputs are finite; a program needn't handle non-finite values.
Results may differ from a plain program's by a relative error of at most 0.001.
Values sent between devices are 32-bit elements.
A program may use at most 1 GiB of HBM per device.

v0:
```python
import math
import jax
import jax.numpy as jnp
from jax import lax
from jax.sharding import PartitionSpec as P

BETA_ONE = 0.9
BETA_TWO = 0.95
ADAM_EPS = 1e-8
WEIGHT_DECAY = 0.1
MAX_NORM = 1.0
CLIP_EPS = 1e-6
STEP = 4
BIAS_ONE = 1.0 - BETA_ONE ** STEP
BIAS_TWO = 1.0 - BETA_TWO ** STEP


def split_flat(flat_vec, shapes):
    tensors = []
    offset = 0
    for piece_shape in shapes:
        piece_size = math.prod(piece_shape)
        tensors.append(flat_vec[offset:offset + piece_size].reshape(piece_shape))
        offset += piece_size
    return tensors


def adam_update(grad_part, grad_norm, master, exp_avg, exp_avg_sq, learn_rate, decay_mask):
    clip_coef = jnp.minimum(1.0, MAX_NORM / (grad_norm + CLIP_EPS))
    clipped = clip_coef * grad_part
    new_avg = BETA_ONE * exp_avg + (1.0 - BETA_ONE) * clipped
    new_avg_sq = BETA_TWO * exp_avg_sq + (1.0 - BETA_TWO) * clipped * clipped
    adam_dir = (new_avg / BIAS_ONE) / (jnp.sqrt(new_avg_sq / BIAS_TWO) + ADAM_EPS)
    decay_term = jnp.where(decay_mask, WEIGHT_DECAY * master, 0.0)
    new_master = master - learn_rate * (decay_term + adam_dir)
    return new_master, new_avg, new_avg_sq


def solution(mesh):
    num_devices = mesh.shape["dp"]

    def optimizer_step(*arrays):
        shapes = [grad_array.shape[1:] for grad_array in arrays[:10]]
        counts = [math.prod(piece_shape) for piece_shape in shapes]
        total_count = sum(counts)
        matrix_count = sum(counts[:7])
        padded = arrays[10].shape[0]
        shard_len = padded // num_devices

        def local_step(*local_arrays):
            local_grads = local_arrays[:10]
            master, exp_avg, exp_avg_sq, learn_rate = local_arrays[10:]
            pieces = [local_grad.reshape(-1).astype(jnp.float32) for local_grad in local_grads]
            pieces.append(jnp.zeros((padded - total_count,), jnp.float32))
            local_flat = jnp.concatenate(pieces)
            grad_shard = lax.psum_scatter(local_flat, "dp", scatter_dimension=0, tiled=True) / num_devices
            grad_norm = jnp.sqrt(lax.psum(jnp.sum(grad_shard * grad_shard), "dp"))
            shard_start = lax.axis_index("dp") * shard_len
            decay_mask = (shard_start + jnp.arange(shard_len)) < matrix_count
            new_master, new_avg, new_avg_sq = adam_update(grad_shard, grad_norm, master, exp_avg, exp_avg_sq, learn_rate, decay_mask)
            full_master = lax.all_gather(new_master, "dp", tiled=True)
            params = split_flat(full_master[:total_count].astype(jnp.bfloat16), shapes)
            return tuple([new_master, new_avg, new_avg_sq] + params + [grad_norm])

        mapped = jax.shard_map(local_step, mesh=mesh, in_specs=(P("dp"),) * 13 + (P(),), out_specs=(P("dp"),) * 3 + (P(),) * 11, check_vma=False)
        return mapped(*arrays)

    return optimizer_step
```

profile of v0, /device:TPU:0, one launch (start us, length us, event | category | flops | bytes accessed | tf_op | source)
XLA Modules:
  0.0 2380.0 jit_solution(15373810175571540756)
XLA Ops:
  7.2 0.0 copy-start
  7.2 0.0 all-reduce.3.cloned.1.call-start
  7.2 7.3 reshape.95
  14.5 4.8 constant_dynamic-update-slice_fusion.8
  19.3 0.0 copy-done
  19.3 5.6 reshape.98
  24.9 35.2 %reshape.99 = f32[8716288]{0:T(1024)} reshape(bf16[1,2,896,4864]{3,2,1,0:T(8,128)(2,1)} %param.18) | data formatting | bytes 52297728 | tf_op jit(solution)/shard_map/convert_element_type | solution.py:53
  60.1 35.3 %reshape.100 = f32[8716288]{0:T(1024)} reshape(bf16[1,2,896,4864]{3,2,1,0:T(8,128)(2,1)} %param.19) | data formatting | bytes 52297728 | tf_op jit(solution)/shard_map/convert_element_type | solution.py:53
  95.3 0.0 copy-start.3
  95.3 0.0 copy-start.4
  95.3 0.0 copy-start.5
  95.3 0.0 copy-start.1
  95.3 0.0 copy-start.2
  95.4 33.8 %reshape.101 = f32[8716288]{0:T(1024)} reshape(bf16[1,2,4864,896]{3,2,1,0:T(8,128)(2,1)} %param.20) | data formatting | bytes 52297728 | tf_op jit(solution)/shard_map/convert_element_type | solution.py:53
  129.2 0.0 copy-done.3
  129.2 0.0 copy-done.4
  129.2 0.0 copy-done.5
  129.3 0.0 copy-done.1
  129.3 1.0 convert_dynamic-update-slice_fusion.1
  130.3 0.0 copy-done.2
  130.3 1.0 convert_dynamic-update-slice_fusion
  131.3 4.9 constant_dynamic-update-slice_fusion.7
  136.1 23.6 constant_dynamic-update-slice_fusion.6
  159.7 23.6 constant_dynamic-update-slice_fusion.5
  183.3 23.6 constant_dynamic-update-slice_fusion.4
  206.9 1.3 constant_dynamic-update-slice_fusion.3
  208.2 1.3 constant_dynamic-update-slice_fusion.2
  209.5 1.3 constant_dynamic-update-slice_fusion.1
  210.8 1.3 constant_dynamic-update-slice_fusion
  212.1 0.0 all-reduce.3.cloned.1.call-update
  212.1 0.0 all-gather.3.cloned.1.call-start
  212.8 1308.5 %all-reduce.3.cloned.1.call-done = f32[29824000]{0:T(1024)} async-done(((f32[29824000]{0:T(1024)}), f32[29824000]{0:T(1024)}) %all-reduce.3.cloned.1.call-update) | async-done | bytes 119296016
  1521.3 8.2 multiply_reduce_fusion
  1529.5 22.6 psum.7
  1552.8 34.5 %multiply_subtract_fusion = (f32[3728000]{0:T(1024)}, f32[3728000]{0:T(1024)}, f32[3728000]{0:T(1024)}) fusion(f32[3728000]{0:T(1024)} %param.24, s32[]{:T(128)S(6)} %mul.48, f32[]{:T(128)S(6)} %copy.39, f32[]{:T(128)S(6)} %mul.53, f32[29824000]{0:T(1024)} %all-reduce.3.cloned.1.call-done, u32[]{:T(128)S(6)} %multiply.6, f32[3728000]{0:T(1024)} %param.25, ...), kind=kLoop, calls=%fused_computation.3 | loop fusion | flops 70832000 | bytes 104384016 | tf_op jit(solution)/shard_map/sub | solution.py:35
  1587.4 56.8 %reshape.105 = f32[1,1,3728000]{2,1,0:T(1,128)} reshape(f32[3728000]{0:T(1024)} %get-tuple-element.14) | data formatting | bytes 29824000
  1644.2 0.0 all-gather.3.cloned.1.call-update
  1644.2 520.4 %all-gather.3.cloned.1.call-done = f32[8,1,3728000]{2,1,0:T(1,128)} async-done(((f32[1,1,3728000]{2,1,0:T(1,128)}), f32[8,1,3728000]{2,1,0:T(1,128)}) %all-gather.3.cloned.1.call-update) | async-done | bytes 119296016 | tf_op jit(solution)/shard_map/all_gather | solution.py:61
  2164.7 57.5 %slice.66 = bf16[29823360]{0:T(1024)(128)(2,1)} slice(f32[29824000]{0:T(1024)} %bitcast.2), slice={[0:29823360]} | slice | bytes 119293440 | tf_op jit(solution)/shard_map/slice | solution.py:62
  2222.2 35.0 %fusion.3 = (bf16[8716288]{0:T(1024)(128)(2,1)}, bf16[8716288]{0:T(1024)(128)(2,1)}, bf16[8716288]{0:T(1024)(128)(2,1)}) fusion(bf16[29823360]{0:T(1024)(128)(2,1)} %slice.66), kind=kLoop, calls=%fused_computation.20 | loop fusion | bytes 104595456 | tf_op jit(solution)/shard_map/slice | solution.py:23
  2257.2 4.2 fusion.4
  2261.5 2.1 fusion.5
  2263.6 0.8 fusion.2
  2264.4 1.2 slice.64
  2265.6 31.5 %reshape.92 = bf16[2,896,4864]{2,1,0:T(8,128)(2,1)} reshape(bf16[8716288]{0:T(1024)(128)(2,1)} %get-tuple-element.21) | data formatting | bytes 34865152 | tf_op jit(solution)/shard_map/reshape | solution.py:23
  2297.1 31.5 %reshape.93 = bf16[2,896,4864]{2,1,0:T(8,128)(2,1)} reshape(bf16[8716288]{0:T(1024)(128)(2,1)} %get-tuple-element.20) | data formatting | bytes 34865152 | tf_op jit(solution)/shard_map/reshape | solution.py:23
  2328.6 31.4 %reshape.94 = bf16[2,4864,896]{2,1,0:T(8,128)(2,1)} reshape(bf16[8716288]{0:T(1024)(128)(2,1)} %get-tuple-element.19) | data formatting | bytes 34865152 | tf_op jit(solution)/shard_map/reshape | solution.py:23
  2360.0 6.7 reshape.88
  2366.7 4.2 reshape.91
  2370.9 0.6 slice.50
  2371.5 0.6 slice.52
  (3 shorter events, 0.0 us)
Async XLA Ops:
  7.2 12.1 copy-start
  7.2 1514.1 %all-reduce.3.cloned.1.call-start = ((), (), s32[]{:S(2)}) async-start(), calls=%async_computation.1 | async-start | bytes 238592000
  95.3 33.9 %copy-start.3 = (bf16[1,2,896]{2,1,0:T(2,128)(2,1)S(1)}, bf16[1,2,896]{2,1,0:T(2,128)(2,1)}, u32[]{:S(2)}) copy-start(bf16[1,2,896]{2,1,0:T(2,128)(2,1)} %param.21) | copy-start | bytes 10756
  95.3 33.9 %copy-start.4 = (bf16[1,2,896]{2,1,0:T(2,128)(2,1)S(1)}, bf16[1,2,896]{2,1,0:T(2,128)(2,1)}, u32[]{:S(2)}) copy-start(bf16[1,2,896]{2,1,0:T(2,128)(2,1)} %param.22) | copy-start | bytes 10756
  95.3 33.9 %copy-start.5 = (bf16[1,896]{1,0:T(2,128)(2,1)S(1)}, bf16[1,896]{1,0:T(2,128)(2,1)}, u32[]{:S(2)}) copy-start(bf16[1,896]{1,0:T(2,128)(2,1)} %param.23) | copy-start | bytes 5380
  95.3 33.9 %copy-start.1 = (bf16[1,2,896,128]{3,2,1,0:T(8,128)(2,1)S(1)}, bf16[1,2,896,128]{3,2,1,0:T(8,128)(2,1)}, u32[]{:S(2)}) copy-start(bf16[1,2,896,128]{3,2,1,0:T(8,128)(2,1)} %param.15) | copy-start | bytes 1376260
  95.3 34.9 %copy-start.2 = (bf16[1,2,896,128]{3,2,1,0:T(8,128)(2,1)S(1)}, bf16[1,2,896,128]{3,2,1,0:T(8,128)(2,1)}, u32[]{:S(2)}) copy-start(bf16[1,2,896,128]{3,2,1,0:T(8,128)(2,1)} %param.16) | copy-start | bytes 1376260
  212.1 1952.5 %all-gather.3.cloned.1.call-start = ((), (), s32[]{:S(2)}) async-start(), calls=%async_computation | async-start | bytes 134208000 | tf_op jit(solution)/shard_map/all_gather | solution.py:61
Sparse Core Ops, SparseCore 0:
  212.2 1309.0 all-reduce.2
  1644.3 520.2 all-gather.2
where the time goes:
time: 2390 us; the launch traced here: 2380 us
  waiting for transfers between devices  1830 us (77%)
  local copies, waits for them, and re-layouts  467 us (20%)
  other arithmetic  44.7 us (2%)
    unnamed x3, waiting for transfers between devices  1310 us
    all_gather x1, waiting for transfers between devices, local_step(): full_master = lax.all_gather(new_master, 'dp', tiled=True)  520 us
    unnamed x21, local copies, waits for them, and re-layouts  141 us
    convert_element_type x7, local copies, waits for them, and re-layouts, local_step(): local_grad.reshape(-1).astype(jnp.float32)  117 us
    reshape x5, local copies, waits for them, and re-layouts, split_flat(): tensors.append(flat_vec[offset:offset + piece_size].reshape(piece_shape))  105 us
    slice x1, local copies, waits for them, and re-layouts, local_step(): params = split_flat(full_master[:total_count].astype(jnp.bfloat16), shapes)  57.5 us
  transfers between devices with their start and end apart: 2, of which 2 were waited for; matrix products, arithmetic and copies ran while one was open for 0% of the time, Pallas kernels for 0%

commit v1 on v0

v1 whole, which is shorter than its diff:
```python
import functools
import math
import jax
import jax.numpy as jnp
from jax import lax
from jax.experimental import pallas as pl
from jax.experimental.pallas import tpu as pltpu
from jax.sharding import PartitionSpec as P

BETA_ONE = 0.9
BETA_TWO = 0.95
ADAM_EPS = 1e-8
WEIGHT_DECAY = 0.1
MAX_NORM = 1.0
CLIP_EPS = 1e-6
STEP = 4
BIAS_ONE = 1.0 - BETA_ONE ** STEP
BIAS_TWO = 1.0 - BETA_TWO ** STEP

MESH = pl.DeviceIdType.MESH
F32 = jnp.float32
BF16 = jnp.bfloat16
LANES = 128

SHAPES = [(2, 896, 896), (2, 896, 128), (2, 896, 128), (2, 896, 896), (2, 896, 4864), (2, 896, 4864), (2, 4864, 896)]
NAMES_ROWS = [math.prod(s[:-1]) for s in SHAPES]
WIDTHS = [s[-1] // LANES for s in SHAPES]
OFFSETS = [sum(r * w for r, w in zip(NAMES_ROWS[:t], WIDTHS[:t])) for t in range(7)]
BLOCK_ROWS = [448, 1792, 1792, 448, 128, 128, 608]
MATRIX_ROWS = 232960
FLAT_ROWS = 233000
SEG = 29125
NDEV = 8

BLOCKS = [(t, b, BLOCK_ROWS[t]) for t in range(7) for b in range(0, NAMES_ROWS[t], BLOCK_ROWS[t])]
STAGE_ROWS = max(br * WIDTHS[t] for t, br in enumerate(BLOCK_ROWS))

ANY = pl.BlockSpec(memory_space=pl.ANY)
VMEM_SPEC = pl.BlockSpec(memory_space=pltpu.VMEM)
SMEM_SPEC = pl.BlockSpec(memory_space=pltpu.SMEM)
DMA = pltpu.SemaphoreType.DMA


def tile_scratch(slots, dtype):
    return [pltpu.VMEM((slots, 128, 4864), dtype), pltpu.VMEM((slots, 608, 896), dtype), pltpu.VMEM((slots, 1792, 128), dtype)]


def width_slot(width):
    return {38: 0, 7: 1, 1: 2}[width]


def pack_kernel(*refs):
    grads, norms, flat = refs[:7], refs[7:10], refs[10]
    tiles, stage, tail, in_sem, out_sem, tail_sem = refs[11:14], refs[14], refs[15], refs[16], refs[17], refs[18]

    def load(b):
        t, row, rows = BLOCKS[b]
        return pltpu.make_async_copy(grads[t].at[pl.ds(row, rows)], tiles[width_slot(WIDTHS[t])].at[b % 2, pl.ds(0, rows)], in_sem.at[b % 2])

    def store(b):
        t, row, rows = BLOCKS[b]
        w = WIDTHS[t]
        return pltpu.make_async_copy(stage.at[b % 2, pl.ds(0, rows * w)], flat.at[pl.ds(OFFSETS[t] + row * w, rows * w), 0], out_sem.at[b % 2])

    load(0).start()
    load(1).start()
    tail[...] = jnp.zeros_like(tail)
    for n, base in ((0, 0), (1, 14)):
        for layer in range(2):
            for j in range(7):
                tail[base + layer * 7 + j:base + layer * 7 + j + 1, :] = norms[n][layer:layer + 1, j * LANES:(j + 1) * LANES].astype(F32)
    for j in range(7):
        tail[28 + j:29 + j, :] = norms[2][:, j * LANES:(j + 1) * LANES].astype(F32)
    tail_copy = pltpu.make_async_copy(tail, flat.at[pl.ds(MATRIX_ROWS, 40), 0], tail_sem)
    tail_copy.start()
    for b, (t, row, rows) in enumerate(BLOCKS):
        w = WIDTHS[t]
        tile = tiles[width_slot(w)]
        group = 16 if w == 38 else (32 if w == 7 else 128)
        load(b).wait()
        if b >= 2:
            store(b - 2).wait()

        @pl.loop(0, rows // group)
        def _(i):
            for j in range(w):
                block = tile[b % 2, pl.ds(pl.multiple_of(i * group, 16), group), j * LANES:(j + 1) * LANES].astype(F32)
                if w == 1:
                    stage[b % 2, pl.ds(pl.multiple_of(i * group, 16), group), :] = block
                else:
                    stage[b % 2, pl.ds(i * (group * w) + j, group, stride=w), :] = block

        store(b).start()
        if b + 2 < len(BLOCKS):
            load(b + 2).start()
    tail_copy.wait()
    store(len(BLOCKS) - 2).wait()
    store(len(BLOCKS) - 1).wait()


def pack(grads, norms):
    return pl.pallas_call(
        pack_kernel,
        name="pack",
        out_shape=jax.ShapeDtypeStruct((FLAT_ROWS, 1, LANES), F32),
        in_specs=[ANY] * 7 + [VMEM_SPEC] * 3,
        out_specs=ANY,
        scratch_shapes=tile_scratch(2, BF16) + [pltpu.VMEM((2, STAGE_ROWS, LANES), F32), pltpu.VMEM((40, LANES), F32), DMA((2,)), DMA((2,)), DMA],
        compiler_params=pltpu.CompilerParams(vmem_limit_bytes=40 * 1024 * 1024),
        cost_estimate=pl.CostEstimate(flops=FLAT_ROWS * 128, bytes_accessed=FLAT_ROWS * 128 * 6, transcendentals=0),
    )(*grads, *norms)


def unpack_kernel(flat, *refs):
    outs, norms = refs[:7], refs[7:10]
    tiles, stage, tail, in_sem, out_sem, tail_sem = refs[10:13], refs[13], refs[14], refs[15], refs[16], refs[17]

    def load(b):
        t, row, rows = BLOCKS[b]
        w = WIDTHS[t]
        return pltpu.make_async_copy(flat.at[pl.ds(OFFSETS[t] + row * w, rows * w), 0], stage.at[b % 2, pl.ds(0, rows * w)], in_sem.at[b % 2])

    def store(b):
        t, row, rows = BLOCKS[b]
        return pltpu.make_async_copy(tiles[width_slot(WIDTHS[t])].at[b % 2, pl.ds(0, rows)], outs[t].at[pl.ds(row, rows)], out_sem.at[b % 2])

    tail_copy = pltpu.make_async_copy(flat.at[pl.ds(MATRIX_ROWS, 40), 0], tail, tail_sem)
    tail_copy.start()
    load(0).start()
    load(1).start()
    tail_copy.wait()
    for n, base in ((0, 0), (1, 14)):
        for j in range(7):
            pair = jnp.concatenate([tail[base + j:base + j + 1, :], tail[base + 7 + j:base + 8 + j, :]], axis=0)
            norms[n][:, j * LANES:(j + 1) * LANES] = pair.astype(BF16)
    for j in range(7):
        norms[2][:, j * LANES:(j + 1) * LANES] = tail[28 + j:29 + j, :].astype(BF16)
    for b, (t, row, rows) in enumerate(BLOCKS):
        w = WIDTHS[t]
        tile = tiles[width_slot(w)]
        group = 16 if w == 38 else (32 if w == 7 else 128)
        load(b).wait()
        if b >= 2:
            store(b - 2).wait()

        @pl.loop(0, rows // group)
        def _(i):
            for j in range(w):
                if w == 1:
                    block = stage[b % 2, pl.ds(pl.multiple_of(i * group, 16), group), :]
                else:
                    block = stage[b % 2, pl.ds(i * (group * w) + j, group, stride=w), :]
                tile[b % 2, pl.ds(pl.multiple_of(i * group, 16), group), j * LANES:(j + 1) * LANES] = block.astype(BF16)

        store(b).start()
        if b + 2 < len(BLOCKS):
            load(b + 2).start()
    store(len(BLOCKS) - 2).wait()
    store(len(BLOCKS) - 1).wait()


def unpack(flat):
    shapes = [jax.ShapeDtypeStruct((r, w * LANES), BF16) for r, w in zip(NAMES_ROWS, WIDTHS)]
    shapes += [jax.ShapeDtypeStruct((2, 896), BF16)] * 2 + [jax.ShapeDtypeStruct((1, 896), BF16)]
    return pl.pallas_call(
        unpack_kernel,
        name="unpack",
        out_shape=shapes,
        in_specs=[ANY],
        out_specs=[ANY] * 7 + [VMEM_SPEC] * 3,
        scratch_shapes=tile_scratch(2, BF16) + [pltpu.VMEM((2, STAGE_ROWS, LANES), F32), pltpu.VMEM((40, LANES), F32), DMA((2,)), DMA((2,)), DMA],
        compiler_params=pltpu.CompilerParams(vmem_limit_bytes=40 * 1024 * 1024),
        cost_estimate=pl.CostEstimate(flops=FLAT_ROWS * 128, bytes_accessed=FLAT_ROWS * 128 * 6, transcendentals=0),
    )(flat)


def neighbours():
    me = lax.axis_index("dp")
    core, x, y = lax.rem(me, 2), lax.rem(me // 2, 2), me // 4
    other = 1 - 2 * core
    step_x, step_y = 2 - 4 * x, 4 - 8 * y
    return me, other, me + step_x, me + step_y, me + step_x + step_y


RS_ROWS = 1821
RS_HALF_START = SEG - 8 * RS_ROWS
KIND_D, KIND_N, KIND_S, KIND_O = range(4)


def reduce_kernel(flat, g_out, norm_out, land_p, land_d, land_n, land_s,
                  mine, part, first, second, sums, g_buf, ss, ss_all,
                  p_send, p_recv, i_send, i_recv, load_sem, g_sem, ss_send, ss_recv):
    me, other, dev_x, dev_y, dev_d = neighbours()
    barrier = pltpu.get_barrier_semaphore()
    for d in range(1, NDEV):
        pl.semaphore_signal(barrier, inc=1, device_id=(lax.rem(me + d, NDEV),), device_id_type=MESH)
    pl.semaphore_wait(barrier, NDEV - 1)

    def segment(kind, h):
        return ((dev_d, dev_d), (dev_x, dev_y), (dev_y, dev_x), (me, me))[kind][h]

    def start_row(h, i):
        return RS_HALF_START * h + RS_ROWS * i

    def partner_copy(kind, h, i):
        row = SEG * (segment(kind, h) + other) + start_row(h, i)
        return pltpu.make_async_remote_copy(
            src_ref=flat.at[pl.ds(row, RS_ROWS)], dst_ref=land_p.at[kind, h, i],
            send_sem=p_send.at[kind, h, i], recv_sem=p_recv.at[kind, h, i],
            device_id=(me + other,), device_id_type=MESH)

    def link_copy(kind, h, i):
        land = (land_d, land_n, land_s)[kind]
        to = ((dev_x, dev_y), (dev_x, dev_y), (dev_y, dev_x))[kind][h]
        return pltpu.make_async_remote_copy(
            src_ref=sums.at[kind, h, i], dst_ref=land.at[h, i, pl.ds(0, RS_ROWS), 0],
            send_sem=i_send.at[kind, h, i], recv_sem=i_recv.at[kind, h, i],
            device_id=(to,), device_id_type=MESH)

    def load_mine(kind, h, i):
        row = SEG * segment(kind, h) + start_row(h, i)
        return pltpu.make_async_copy(flat.at[pl.ds(row, RS_ROWS), 0], mine.at[h], load_sem.at[0, h])

    def load_part(kind, h, i):
        return pltpu.make_async_copy(land_p.at[kind, h, i, pl.ds(0, RS_ROWS), 0], part.at[h], load_sem.at[1, h])

    def load_link(land, buf, n, h, i):
        return pltpu.make_async_copy(land.at[h, i, pl.ds(0, RS_ROWS), 0], buf.at[h], load_sem.at[n, h])

    def store_g(h, i):
        return pltpu.make_async_copy(g_buf.at[h], g_out.at[pl.ds(start_row(h, i), RS_ROWS), 0], g_sem.at[h])

    @pl.loop(0, 8)
    def _(i):
        for h in range(2):
            partner_copy(KIND_D, h, i).start()

    for kind in (KIND_D, KIND_N, KIND_S):
        @pl.loop(0, 8)
        def _(i):
            for h in range(2):
                load_mine(kind, h, i).start()
                partner_copy(kind + 1, h, i).start()
            for h in range(2):
                partner_copy(kind, h, i).wait_recv()
                load_part(kind, h, i).start()
                if kind == KIND_S:
                    link_copy(KIND_D, h, i).wait_recv()
                    load_link(land_d, first, 2, h, i).start()
            for h in range(2):
                load_mine(kind, h, i).wait()
                load_part(kind, h, i).wait()
                total = mine[h] + part[h]
                if kind == KIND_S:
                    load_link(land_d, first, 2, h, i).wait()
                    total = total + first[h]
                sums[kind, h, i] = total
                link_copy(kind, h, i).start()

    def last(i, acc):
        for h in range(2):
            load_mine(KIND_O, h, i).start()
            partner_copy(KIND_O, h, i).wait_recv()
            load_part(KIND_O, h, i).start()
        for h in range(2):
            link_copy(KIND_N, h, i).wait_recv()
            load_link(land_n, first, 2, h, i).start()
        for h in range(2):
            link_copy(KIND_S, h, i).wait_recv()
            load_link(land_s, second, 3, h, i).start()
            load_mine(KIND_O, h, i).wait()
            load_part(KIND_O, h, i).wait()
            load_link(land_n, first, 2, h, i).wait()
            load_link(land_s, second, 3, h, i).wait()

            @pl.when(i > 0)
            def _():
                store_g(h, i - 1).wait()

            g = ((mine[h] + part[h]) + (first[h] + second[h])) * (1.0 / NDEV)
            g_buf[h] = g
            store_g(h, i).start()
            square = g * g
            if h == 1:
                row = lax.broadcasted_iota(jnp.int32, (RS_ROWS, LANES), 0) + RS_ROWS * i
                square = jnp.where(row >= 8 * RS_ROWS - RS_HALF_START, square, 0.0)
            acc = acc + jnp.sum(square, axis=0, keepdims=True)
        return acc

    acc = lax.fori_loop(0, 8, last, jnp.zeros((1, LANES), F32))
    ss[...] = jnp.broadcast_to(acc, (8, LANES))
    for h in range(2):
        store_g(h, 7).wait()

    @pl.loop(0, 8)
    def _(i):
        for h in range(2):
            for kind in range(4):
                partner_copy(kind, h, i).wait_send()
            for kind in range(3):
                link_copy(kind, h, i).wait_send()

    def norm_copy(d):
        return pltpu.make_async_remote_copy(
            src_ref=ss, dst_ref=ss_all.at[d], send_sem=ss_send.at[d], recv_sem=ss_recv.at[d],
            device_id=(lax.rem(me + d, NDEV),), device_id_type=MESH)

    for d in range(1, NDEV):
        norm_copy(d).start()
    ss_all[0] = ss[...]
    for d in range(1, NDEV):
        norm_copy(d).wait()
    total = jnp.zeros((8, LANES), F32)
    for dev in range(NDEV):
        total = total + ss_all[lax.rem(me - dev + NDEV, NDEV)]
    norm_out[...] = jnp.broadcast_to(jnp.sqrt(jnp.sum(total, axis=1, keepdims=True)), (8, LANES))


def reduce_grads(flat):
    land = jax.ShapeDtypeStruct((2, 8, RS_ROWS, 1, LANES), F32)
    buf = pltpu.VMEM((2, RS_ROWS, LANES), F32)
    outs = pl.pallas_call(
        reduce_kernel,
        name="reduce_grads",
        out_shape=[jax.ShapeDtypeStruct((SEG, 1, LANES), F32), jax.ShapeDtypeStruct((8, LANES), F32),
                   jax.ShapeDtypeStruct((4, 2, 8, RS_ROWS, 1, LANES), F32), land, land, land],
        in_specs=[ANY],
        out_specs=[ANY, VMEM_SPEC, ANY, ANY, ANY, ANY],
        scratch_shapes=[buf, buf, buf, buf, pltpu.VMEM((3, 2, 8, RS_ROWS, LANES), F32), buf,
                        pltpu.VMEM((8, LANES), F32), pltpu.VMEM((NDEV, 8, LANES), F32),
                        DMA((4, 2, 8)), DMA((4, 2, 8)), DMA((3, 2, 8)), DMA((3, 2, 8)), DMA((4, 2)), DMA((2,)), DMA((NDEV,)), DMA((NDEV,))],
        compiler_params=pltpu.CompilerParams(collective_id=0, has_side_effects=True, vmem_limit_bytes=63 * 1024 * 1024),
        cost_estimate=pl.CostEstimate(flops=10 ** 9, bytes_accessed=4 * 10 ** 8, transcendentals=0),
    )(flat)
    return outs[0], outs[1]


def adam_rows(g, m, v, p, norm_row, lr, decay):
    clip = jnp.minimum(1.0, MAX_NORM / (norm_row + CLIP_EPS))
    clipped = clip * g
    new_m = BETA_ONE * m + (1.0 - BETA_ONE) * clipped
    new_v = BETA_TWO * v + (1.0 - BETA_TWO) * clipped * clipped
    adam_dir = (new_m / BIAS_ONE) / (jnp.sqrt(new_v / BIAS_TWO) + ADAM_EPS)
    decay_term = jnp.where(decay, WEIGHT_DECAY * p, 0.0)
    return p - lr * (decay_term + adam_dir), new_m, new_v


UP_ROWS = 1824
UP_LAST = SEG - 15 * UP_ROWS
SUB = 152


def decay_rows(me, start, rows):
    return lax.broadcasted_iota(jnp.int32, (rows, LANES), 0) + (SEG * me + start) < MATRIX_ROWS


def gather_kernel(g, m, v, p, norm, lr, full, gb, mb, vb, pb, new_p,
                  load_sem, own_sem, own_send, own_recv, fwd_send, fwd_recv, p_send, p_recv):
    me, other, dev_x, dev_y, dev_d = neighbours()
    partner = me + other
    barrier = pltpu.get_barrier_semaphore()
    for dev in (partner, dev_x, dev_y):
        pl.semaphore_signal(barrier, inc=1, device_id=(dev,), device_id_type=MESH)
    pl.semaphore_wait(barrier, 3)
    to = (dev_x, dev_y, partner)
    sources = (me, dev_x, dev_y, dev_d)

    def start_row(h, i):
        return UP_ROWS * (8 * h + i)

    def size(h, i):
        return UP_LAST if h == 1 and not isinstance(i, jax.Array) and i == 7 else UP_ROWS

    def rows_of(dev, h, i):
        return full.at[pl.ds(SEG * dev + start_row(h, i), size(h, i)), 0]

    def loads(h, i):
        rows = size(h, i)
        start = pl.multiple_of(start_row(h, i), 8)
        copies = [pltpu.make_async_copy(g.at[pl.ds(start_row(h, i), rows), 0], gb.at[h, pl.ds(0, rows)], load_sem.at[0, h])]
        for n, (src, buf) in enumerate(((m, mb), (v, vb), (p, pb))):
            copies.append(pltpu.make_async_copy(src.at[pl.ds(start, rows)], buf.at[h, pl.ds(0, rows)], load_sem.at[n + 1, h]))
        return copies

    def own_copy(n, h, i):
        return pltpu.make_async_remote_copy(
            src_ref=new_p.at[h, i, pl.ds(0, size(h, i))], dst_ref=rows_of(me, h, i),
            send_sem=own_send.at[n, h, i], recv_sem=own_recv.at[n, h, i], device_id=(to[n],), device_id_type=MESH)

    def own_store(h, i):
        return pltpu.make_async_copy(new_p.at[h, i, pl.ds(0, size(h, i))], rows_of(me, h, i), own_sem.at[h, i])

    def forward(h, i):
        src = rows_of((dev_y, dev_x)[h], h, i)
        return pltpu.make_async_remote_copy(
            src_ref=src, dst_ref=src, send_sem=fwd_send.at[h, i], recv_sem=fwd_recv.at[h, i],
            device_id=((dev_x, dev_y)[h],), device_id_type=MESH)

    def arrival(n, h, i):
        src = rows_of((dev_x, dev_y, partner)[n], h, i)
        return pltpu.make_async_remote_copy(
            src_ref=src, dst_ref=src, send_sem=own_send.at[n, h, i], recv_sem=own_recv.at[n, h, i],
            device_id=(to[n],), device_id_type=MESH)

    def forward_arrival(h, i):
        src = rows_of(dev_d, h, i)
        return pltpu.make_async_remote_copy(
            src_ref=src, dst_ref=src, send_sem=fwd_send.at[h, i], recv_sem=fwd_recv.at[h, i],
            device_id=((dev_x, dev_y)[h],), device_id_type=MESH)

    def partner_copy(q, h, i):
        src = rows_of(sources[q], h, i)
        return pltpu.make_async_remote_copy(
            src_ref=src, dst_ref=src, send_sem=p_send.at[q - 1, h, i], recv_sem=p_recv.at[q - 1, h, i],
            device_id=(partner,), device_id_type=MESH)

    def partner_arrival(q, h, i):
        src = rows_of(sources[q] + other, h, i)
        return pltpu.make_async_remote_copy(
            src_ref=src, dst_ref=src, send_sem=p_send.at[q - 1, h, i], recv_sem=p_recv.at[q - 1, h, i],
            device_id=(partner,), device_id_type=MESH)

    def each(body):
        @pl.loop(0, 7)
        def _(i):
            body(i)

        body(7)

    norm_row = norm[0:1, :]
    for h in range(2):
        for copy in loads(h, 0):
            copy.start()

    def update(i):
        for h in range(2):
            for copy in loads(h, i):
                copy.wait()

            @pl.loop(0, UP_ROWS // SUB)
            def _(s):
                start = pl.multiple_of(s * SUB, 8)
                sub = pl.ds(start, SUB)
                new_p[h, i, sub] = adam_rows(gb[h, sub], mb[h, sub], vb[h, sub], pb[h, sub], norm_row, lr[0],
                                             decay_rows(me, start_row(h, i) + start, SUB))[0]

            for n in ((1, 0, 2) if h == 0 else (0, 1, 2)):
                own_copy(n, h, i).start()
            own_store(h, i).start()
            if isinstance(i, int):
                continue
            for last in (False, True):
                @pl.when((i == 6) == last)
                def _():
                    for copy in loads(h, 7 if last else i + 1):
                        copy.start()

    each(update)

    def pass_on(i):
        arrival(1, 0, i).wait_recv()
        forward(0, i).start()
        partner_copy(2, 0, i).start()
        arrival(0, 1, i).wait_recv()
        forward(1, i).start()
        partner_copy(1, 1, i).start()
        arrival(0, 0, i).wait_recv()
        partner_copy(1, 0, i).start()
        arrival(1, 1, i).wait_recv()
        partner_copy(2, 1, i).start()

    each(pass_on)

    def pass_last(i):
        for h in range(2):
            forward_arrival(h, i).wait_recv()
            partner_copy(3, h, i).start()

    each(pass_last)

    def finish(i):
        for h in range(2):
            own_store(h, i).wait()
            arrival(2, h, i).wait_recv()
            for n in range(3):
                own_copy(n, h, i).wait_send()
            forward(h, i).wait_send()
            for q in range(1, 4):
                partner_copy(q, h, i).wait_send()
                partner_arrival(q, h, i).wait_recv()

    each(finish)


def gather_params(g, m, v, p, norm, lr):
    buf = pltpu.VMEM((2, UP_ROWS, LANES), F32)
    return pl.pallas_call(
        gather_kernel,
        name="gather_params",
        out_shape=jax.ShapeDtypeStruct((FLAT_ROWS, 1, LANES), F32),
        in_specs=[ANY] * 4 + [VMEM_SPEC, SMEM_SPEC],
        out_specs=ANY,
        scratch_shapes=[buf, buf, buf, buf, pltpu.VMEM((2, 8, UP_ROWS, LANES), F32),
                        DMA((4, 2)), DMA((2, 8)), DMA((3, 2, 8)), DMA((3, 2, 8)), DMA((2, 8)), DMA((2, 8)), DMA((3, 2, 8)), DMA((3, 2, 8))],
        compiler_params=pltpu.CompilerParams(collective_id=1, has_side_effects=True, vmem_limit_bytes=48 * 1024 * 1024),
        cost_estimate=pl.CostEstimate(flops=10 ** 9, bytes_accessed=4 * 10 ** 8, transcendentals=0),
    )(g, m, v, p, norm, lr)


def state_kernel(g, m, v, p, norm, lr, new_p, new_m, new_v, gb, g_sem):
    me = lax.axis_index("dp")
    i = pl.program_id(0)

    def load(j, last):
        rows = UP_LAST if last else UP_ROWS
        return pltpu.make_async_copy(g.at[pl.ds(j * UP_ROWS, rows), 0], gb.at[lax.rem(j, 2), pl.ds(0, rows)], g_sem.at[lax.rem(j, 2)])

    @pl.when(i == 0)
    def _():
        load(i, False).start()

    @pl.when(i < 14)
    def _():
        load(i + 1, False).start()

    @pl.when(i == 14)
    def _():
        load(i + 1, True).start()

    @pl.when(i < 15)
    def _():
        load(i, False).wait()

    @pl.when(i == 15)
    def _():
        load(i, True).wait()

    norm_row = norm[0:1, :]

    @pl.loop(0, UP_ROWS // SUB)
    def _(s):
        start = pl.multiple_of(s * SUB, 8)
        rows = pl.ds(start, SUB)
        new_p[rows], new_m[rows], new_v[rows] = adam_rows(
            gb[lax.rem(i, 2), rows], m[rows], v[rows], p[rows], norm_row, lr[0], decay_rows(me, i * UP_ROWS + start, SUB))


def new_state(g, m, v, p, norm, lr):
    block = pl.BlockSpec((UP_ROWS, LANES), lambda i: (i, 0))
    return pl.pallas_call(
        state_kernel,
        name="new_state",
        grid=(16,),
        out_shape=[jax.ShapeDtypeStruct((SEG, LANES), F32)] * 3,
        in_specs=[ANY, block, block, block, pl.BlockSpec((8, LANES), lambda i: (0, 0)), SMEM_SPEC],
        out_specs=[block] * 3,
        scratch_shapes=[pltpu.VMEM((2, UP_ROWS, LANES), F32), DMA((2,))],
        compiler_params=pltpu.CompilerParams(vmem_limit_bytes=32 * 1024 * 1024),
        cost_estimate=pl.CostEstimate(flops=20 * SEG * 128, bytes_accessed=28 * SEG * 128, transcendentals=0),
    )(g, m, v, p, norm, lr)


def solution(mesh):
    def local_step(*arrays):
        grads = [a.reshape(r, w * LANES) for a, r, w in zip(arrays[:7], NAMES_ROWS, WIDTHS)]
        norms = [arrays[7].reshape(2, 896), arrays[8].reshape(2, 896), arrays[9].reshape(1, 896)]
        master, exp_avg, exp_avg_sq = [a.reshape(SEG, LANES) for a in arrays[10:13]]
        lr = arrays[13].reshape(1)
        flat = pack(grads, norms)
        g, norm = reduce_grads(flat)
        full = gather_params(g, exp_avg, exp_avg_sq, master, norm, lr)
        state = new_state(g, exp_avg, exp_avg_sq, master, norm, lr)
        params = unpack(full)
        shapes = SHAPES + [(2, 896), (2, 896), (896,)]
        return tuple([a.reshape(-1) for a in state] + [a.reshape(s) for a, s in zip(params, shapes)] + [norm[0, 0]])

    return jax.shard_map(local_step, mesh=mesh, in_specs=(P("dp"),) * 13 + (P(),), out_specs=(P("dp"),) * 3 + (P(),) * 11, check_vma=False)
```

time: 2390 us -> 1190 us (0.50)
  waiting for transfers between devices: 1830 us -> 0 us
  Pallas kernels: 0 us -> 1170 us
  local copies, waits for them, and re-layouts: 467 us -> 14.3 us
  other arithmetic: 44.7 us -> 0.6 us
    unnamed x3 -> x0, waiting for transfers between devices: 1310 us -> none
    pallas_call x0 -> x5, Pallas kernels: none -> 1170 us  [the longest x1 501 us: reduce_grads(): pl.pallas_call(reduce_kernel, name='reduce_grads', out_shape=[jax.ShapeDt...]
    all_gather x1 -> x0, waiting for transfers between devices: 520 us -> none  [local_step(): full_master = lax.all_gather(new_master, 'dp', tiled=True)]
    unnamed x21 -> x20, local copies, waits for them, and re-layouts: 141 us -> 13.8 us
    convert_element_type x7 -> x0, local copies, waits for them, and re-layouts: 117 us -> none  [local_step(): local_grad.reshape(-1).astype(jnp.float32)]
    reshape x5 -> x0, local copies, waits for them, and re-layouts: 105 us -> none  [split_flat(): tensors.append(flat_vec[offset:offset + piece_size].reshape(piece_shape))]
    slice x8 -> x1, local copies, waits for them, and re-layouts: 102 us -> 0.51 us  [local_step(): norm[0, 0]]
    sub x1 -> x0, other arithmetic: 34.5 us -> none  [adam_update(): new_master = master - learn_rate * (decay_term + adam_dir)]
  transfers between devices with their start and end apart: 2 -> 0, of which waited for: 2 -> 0; matrix products, arithmetic and copies ran while one was open for 0% -> 0% of each run, Pallas kernels for 0% -> 0%
where the time goes in v1:
time: 1190 us; the launch traced here: 1180 us
  Pallas kernels  1170 us (98%)
  local copies, waits for them, and re-layouts  14.3 us (1%)
    pallas_call x1, Pallas kernels, reduce_grads(): pl.pallas_call(reduce_kernel, name='reduce_grads', out_shape=[jax.ShapeDt...  501 us
    pallas_call x1, Pallas kernels, gather_params(): pl.pallas_call(gather_kernel, name='gather_params', out_shape=jax.ShapeDt...  491 us
    pallas_call x1, Pallas kernels, unpack(): pl.pallas_call(unpack_kernel, name='unpack', out_shape=shapes, in_specs=[...  75.3 us
    pallas_call x1, Pallas kernels, pack(): pl.pallas_call(pack_kernel, name='pack', out_shape=jax.ShapeDtypeStruct((...  59.7 us
    pallas_call x1, Pallas kernels, new_state(): pl.pallas_call(state_kernel, name='new_state', grid=(16,), out_shape=[jax...  41.4 us

profile of v1, /device:TPU:0, one launch (start us, length us, event | category | flops | bytes accessed | tf_op | source)
XLA Modules:
  0.0 1184.6 jit_solution(14360147923605793048)
XLA Ops:
  0.6 0.0 copy-start.1
  0.7 1.9 copy-done.1
  2.6 0.0 copy-start.2
  2.6 1.9 copy-done.2
  4.5 0.0 copy-start.3
  4.5 1.0 copy-done.3
  5.5 0.0 copy-start.4
  5.5 1.0 copy-done.4
  6.5 0.0 copy-start.7
  6.5 0.7 copy-done.7
  7.2 0.0 copy-start.8
  7.2 0.7 copy-done.8
  7.9 0.0 copy-start.9
  7.9 0.7 copy-done.9
  8.6 59.7 %pack.1.flat = f32[233000,1,128]{2,1,0:T(1,128)} custom-call(bf16[1792,896]{1,0:T(8,128)(2,1)S(1)} %bitcast.26, bf16[1792,128]{1,0:T(8,128)(2,1)S(1)} %bitcast.28, bf16[1792,128]{1,0:T(8,128)(2,1)S(1)} %bitcast.29, bf16[1792,896]{1,0:T(8,128)(2,1)S(1)} %bitcast.27, bf16[1792,4864]{1,0:T(8,128)(2,1)} %bitcast.38, bf16[1792,4864]{1,0:T(8,128)(2,1)} %bitcast.39, ...), custom_call_target="tpu_custom_call" | custom-call | flops 29824000 | bytes 178944000 | tf_op jit(solution)/shard_map/pack/pallas_call | solution.py:102
  68.3 500.7 %reduce_grads.1 = (f32[29125,1,128]{2,1,0:T(1,128)}, f32[8,128]{1,0:T(8,128)}, f32[4,2,8,1821,1,128]{5,4,3,2,1,0:T(1,128)}, f32[2,8,1821,1,128]{4,3,2,1,0:T(1,12...) custom-call(f32[233000,1,128]{2,1,0:T(1,128)} %pack.1.flat), custom_call_target="tpu_custom_call" | custom-call | flops 1000000000 | bytes 400000000 | tf_op jit(solution)/shard_map/reduce_grads/pallas_call | solution.py:322
  569.6 0.0 copy-start.5
  569.6 0.7 copy-done.5
  570.3 491.2 %gather_params.1.flat = f32[233000,1,128]{2,1,0:T(1,128)} custom-call(f32[29125,1,128]{2,1,0:T(1,128)} %get-tuple-element.29.g, f32[29125,128]{1,0:T(8,128)} %bitcast.32, f32[29125,128]{1,0:T(8,128)} %bitcast.34, f32[29125,128]{1,0:T(8,128)} %bitcast.36, f32[8,128]{1,0:T(8,128)S(1)} %copy-done.5, f32[1]{0:T(128)} %bitcast.25.lr), custom_call_target="tpu_custom_call" | custom-call | flops 1000000000 | bytes 400000000 | tf_op jit(solution)/shard_map/gather_params/pallas_call | solution.py:497
  1061.5 0.0 copy-start.6
  1061.5 75.3 %unpack.1 = (bf16[1792,896]{1,0:T(8,128)(2,1)}, bf16[1792,128]{1,0:T(8,128)(2,1)}, bf16[1792,128]{1,0:T(8,128)(2,1)}, bf16[1792,896]{1,0:T(8,128)(2,1)}, bf16[17...) custom-call(f32[233000,1,128]{2,1,0:T(1,128)} %gather_params.1.flat), custom_call_target="tpu_custom_call" | custom-call | flops 29824000 | bytes 178944000 | tf_op jit(solution)/shard_map/unpack/pallas_call | solution.py:165
  1136.8 0.6 reduce
  1137.4 0.0 copy-done.6
  1137.4 0.0 copy-start
  1137.4 5.2 copy-done
  1142.7 41.4 %new_state.1 = (f32[29125,128]{1,0:T(8,128)}, f32[29125,128]{1,0:T(8,128)}, f32[29125,128]{1,0:T(8,128)}) custom-call(f32[29125,1,128]{2,1,0:T(1,128)S(1)} %copy-done, f32[29125,128]{1,0:T(8,128)} %bitcast.33, f32[29125,128]{1,0:T(8,128)} %bitcast.35, f32[29125,128]{1,0:T(8,128)} %bitcast.37, f32[8,128]{1,0:T(8,128)S(1)} %copy-done.6, f32[1]{0:T(128)} %bitcast.24.lr), custom_call_target="tpu_custom_call" | custom-call | flops 74560000 | bytes 104384000 | tf_op jit(solution)/shard_map/new_state/pallas_call | solution.py:550
  1184.1 0.5 slice.3
Async XLA Ops:
  0.6 1.9 copy-start.1
  2.6 1.9 copy-start.2
  4.5 1.0 copy-start.3
  5.5 1.0 copy-start.4
  6.5 0.7 copy-start.7
  7.2 0.7 copy-start.8
  7.9 0.7 copy-start.9
  569.6 0.7 copy-start.5
  1061.5 75.9 %copy-start.6 = (f32[8,128]{1,0:T(8,128)S(1)}, f32[8,128]{1,0:T(8,128)}, u32[]{:S(2)}) copy-start(f32[8,128]{1,0:T(8,128)} %get-tuple-element.30.norm) | copy-start | bytes 12292
  1137.4 5.2 copy-start

commit v2 on v1

v2 whole, which is shorter than its diff:
```python
import functools
import math
import jax
import jax.numpy as jnp
from jax import lax
from jax.experimental import pallas as pl
from jax.experimental.pallas import tpu as pltpu
from jax.sharding import PartitionSpec as P

BETA_ONE = 0.9
BETA_TWO = 0.95
ADAM_EPS = 1e-8
WEIGHT_DECAY = 0.1
MAX_NORM = 1.0
CLIP_EPS = 1e-6
STEP = 4
BIAS_ONE = 1.0 - BETA_ONE ** STEP
BIAS_TWO = 1.0 - BETA_TWO ** STEP

MESH = pl.DeviceIdType.MESH
F32 = jnp.float32
BF16 = jnp.bfloat16
LANES = 128

LAYERS, D, KV, FF = 2, 896, 128, 4864
SHAPES = [(LAYERS, D, D), (LAYERS, D, KV), (LAYERS, D, KV), (LAYERS, D, D), (LAYERS, D, FF), (LAYERS, D, FF), (LAYERS, FF, D)]
GAINS = [(LAYERS, D), (LAYERS, D), (1, D)]
TAIL = 40
HALVES, TENSORS, COLUMNS = range(2), range(7), range(7)
NAMES_ROWS = [math.prod(s[:-1]) for s in SHAPES]
WIDTHS = [s[-1] // LANES for s in SHAPES]
OFFSETS = [sum(r * w for r, w in zip(NAMES_ROWS[:t], WIDTHS[:t])) for t in TENSORS]
BLOCK_ROWS = [448, 1792, 1792, 448, 128, 128, 608]
MATRIX_ROWS = 232960
FLAT_ROWS = 233000
SEG = 29125
NDEV = 8

WIDTH_ORDER = (38, 7, 1)
GROUPS = {38: (16,), 7: (16, 32, 64), 1: (16, 128, 256)}
STAGE_ROWS = max(br * WIDTHS[t] for t, br in enumerate(BLOCK_ROWS))

def split(refs, counts):
    refs = list(refs)
    return [[refs.pop(0) for _ in range(n)] for n in counts]


ANY = pl.BlockSpec(memory_space=pl.ANY)
VMEM_SPEC = pl.BlockSpec(memory_space=pltpu.VMEM)
SMEM_SPEC = pl.BlockSpec(memory_space=pltpu.SMEM)
DMA = pltpu.SemaphoreType.DMA
VMEM_LIMIT = 63 * 1024 * 1024
COST = pl.CostEstimate(flops=2 * 10 ** 8, bytes_accessed=10 ** 8, transcendentals=0)


def tile_scratch(slots, rows):
    return [pltpu.VMEM((slots, r, w * LANES), BF16) for r, w in zip(rows, WIDTH_ORDER)]


def width_slot(width):
    return WIDTH_ORDER.index(width)


def row_group(rows, width):
    return max(g for g in GROUPS[width] if rows % g == 0)


PIECE = 912
PIECES = 32
LATE_FIRST, LATE_END = 25, 31
LATE_ROWS = PIECE * (LATE_END - LATE_FIRST) + 16
PIECE_LAST = SEG - (PIECES - 1) * PIECE
HALF = (PIECES - LATE_END + LATE_FIRST) // 2
LATE_RANGES = [((SEG * s + PIECE * LATE_FIRST) // 8 * 8, -(-(SEG * s + PIECE * LATE_END) // 8) * 8) for s in range(NDEV)]


def unpack_blocks():
    early, late = [], []
    for t in TENSORS:
        w, offset, total = WIDTHS[t], OFFSETS[t], NAMES_ROWS[t]
        cuts = {0, total}
        spans = []
        for low, high in LATE_RANGES:
            first = max(0, (low - offset) // (16 * w) * 16)
            end = min(total, -(-(high - offset) // (16 * w)) * 16)
            if first < end:
                spans.append((first, end))
                cuts |= {first, end}
        cuts = sorted(cuts)
        for begin, end in zip(cuts[:-1], cuts[1:]):
            is_late = any(first <= begin and end <= last for first, last in spans)
            count = -(-(end - begin) // BLOCK_ROWS[t])
            step = -(-(end - begin) // (16 * count)) * 16
            for row in range(begin, end, step):
                rows = min(step, end - row)
                low, high = offset + row * w, offset + (row + rows) * w
                edges = sorted({low, high} | {e for r in LATE_RANGES for e in r if low < e < high})
                sources = []
                for e0, e1 in zip(edges[:-1], edges[1:]):
                    seg = [s for s, (l, h) in enumerate(LATE_RANGES) if l <= e0 and e1 <= h]
                    start = LATE_ROWS * seg[0] + e0 - SEG * seg[0] - PIECE * LATE_FIRST + 8 if seg else e0
                    sources.append((bool(seg), start, e0 - low, e1 - e0))
                (late if is_late else early).append((t, row, rows, sources))
    return early, late


EARLY_BLOCKS, LATE_BLOCKS = unpack_blocks()
LATE_TENSORS = sorted({t for t, _, _, _ in LATE_BLOCKS})
SLOTS = 4


def unpack_body(blocks, sources, outs, tiles, stage, in_sem, out_sem):
    def loads(b):
        return [pltpu.make_async_copy(sources[late].at[pl.ds(start, rows), 0], stage.at[b % SLOTS, pl.ds(to, rows)], in_sem.at[b % SLOTS, n])
                for n, (late, start, to, rows) in enumerate(blocks[b][3])]

    def store(b):
        t, row, rows, _ = blocks[b]
        return pltpu.make_async_copy(tiles[width_slot(WIDTHS[t])].at[b % SLOTS, pl.ds(0, rows)], outs[t].at[pl.ds(row, rows)], out_sem.at[b % SLOTS])

    for b in range(min(SLOTS, len(blocks))):
        for copy in loads(b):
            copy.start()
    yield
    for b, (t, row, rows, _) in enumerate(blocks):
        w = WIDTHS[t]
        tile = tiles[width_slot(w)]
        group = row_group(rows, w)
        for copy in loads(b):
            copy.wait()
        if b >= SLOTS:
            store(b - SLOTS).wait()

        @pl.loop(0, rows // group)
        def _(i):
            for j in range(w):
                if w == 1:
                    block = stage[b % SLOTS, pl.ds(pl.multiple_of(i * group, 16), group), :]
                else:
                    block = stage[b % SLOTS, pl.ds(i * (group * w) + j, group, stride=w), :]
                tile[b % SLOTS, pl.ds(pl.multiple_of(i * group, 16), group), pl.ds(j * LANES, LANES)] = block.astype(BF16)

        store(b).start()
        if b + SLOTS < len(blocks):
            for copy in loads(b + SLOTS):
                copy.start()
    for b in range(max(0, len(blocks) - SLOTS), len(blocks)):
        store(b).wait()


UNPACK_SCRATCH = tile_scratch(SLOTS, (128, 608, 1792)) + [pltpu.VMEM((SLOTS, STAGE_ROWS, LANES), F32)]
TENSOR_TYPES = [jax.ShapeDtypeStruct((r, w * LANES), BF16) for r, w in zip(NAMES_ROWS, WIDTHS)]


def unpack_early_kernel(flat, *refs):
    outs, norms = refs[:7], refs[7:10]
    tiles, stage, tail, in_sem, out_sem, tail_sem = refs[10:13], refs[13], refs[14], refs[15], refs[16], refs[17]
    tail_copy = pltpu.make_async_copy(flat.at[pl.ds(MATRIX_ROWS, TAIL), 0], tail, tail_sem)
    tail_copy.start()
    work = unpack_body(EARLY_BLOCKS, (flat, None), outs, tiles, stage, in_sem, out_sem)
    next(work)
    tail_copy.wait()
    base = 0
    for n in norms:
        for j in COLUMNS:
            lines = [tail[pl.ds(base + j + 7 * layer, 1), :] for layer in range(n.shape[0])]
            n[:, pl.ds(j * LANES, LANES)] = jnp.concatenate(lines, axis=0).astype(BF16)
        base += 7 * n.shape[0]
    for _ in work:
        pass


def unpack_early(flat):
    return pl.pallas_call(
        unpack_early_kernel,
        name="unpack_early",
        out_shape=TENSOR_TYPES + [jax.ShapeDtypeStruct(s, BF16) for s in GAINS],
        in_specs=[ANY],
        out_specs=[ANY] * 7 + [VMEM_SPEC] * 3,
        scratch_shapes=UNPACK_SCRATCH + [pltpu.VMEM((TAIL, LANES), F32), DMA((SLOTS, 3)), DMA((SLOTS,)), DMA],
        compiler_params=pltpu.CompilerParams(vmem_limit_bytes=VMEM_LIMIT),
        cost_estimate=COST,
    )(flat)


def unpack_late_kernel(flat, late, *refs):
    count = len(LATE_TENSORS)
    outs = dict(zip(LATE_TENSORS, refs[count:2 * count]))
    tiles, stage, in_sem, out_sem = refs[2 * count:2 * count + 3], refs[2 * count + 3], refs[2 * count + 4], refs[2 * count + 5]
    for _ in unpack_body(LATE_BLOCKS, (flat, late), outs, tiles, stage, in_sem, out_sem):
        pass


def unpack_late(flat, late, params):
    count = len(LATE_TENSORS)
    outs = pl.pallas_call(
        unpack_late_kernel,
        name="unpack_late",
        out_shape=[TENSOR_TYPES[t] for t in LATE_TENSORS],
        in_specs=[ANY] * (2 + count),
        out_specs=[ANY] * count,
        input_output_aliases={2 + n: n for n in range(count)},
        scratch_shapes=UNPACK_SCRATCH + [DMA((SLOTS, 3)), DMA((SLOTS,))],
        compiler_params=pltpu.CompilerParams(vmem_limit_bytes=VMEM_LIMIT),
        cost_estimate=COST,
    )(flat, late, *[params[t] for t in LATE_TENSORS])
    params = list(params)
    for t, out in zip(LATE_TENSORS, outs):
        params[t] = out
    return params


def neighbours():
    me = lax.axis_index("dp")
    core, x, y = lax.rem(me, 2), lax.rem(me // 2, 2), me // 4
    other = 1 - 2 * core
    step_x, step_y = 2 - 4 * x, 4 - 8 * y
    return me, other, me + step_x, me + step_y, me + step_x + step_y


RS_ROWS = 1821
RS_HALF_START = SEG - 8 * RS_ROWS
KIND_D, KIND_N, KIND_S, KIND_O = range(4)
CHIP_D, CHIP_X, CHIP_Y, CHIP_OWN = range(4)
QUARTER = 4 * RS_ROWS
MARGIN = 16 * 38
PACK_ROWS = {38: 112, 7: 608, 1: 896}
PACK_STAGE = 112 * 38


def pack_blocks(chip, quarter):
    blocks = []
    for parity in HALVES:
        for h in HALVES:
            begin = SEG * (2 * chip + parity) + RS_HALF_START * h + QUARTER * quarter
            for t in TENSORS:
                w, offset, total = WIDTHS[t], OFFSETS[t], NAMES_ROWS[t]
                low, high = max(begin, offset), min(begin + QUARTER, offset + total * w)
                if low >= high:
                    continue
                first = (low - offset) // (16 * w) * 16
                end = -(-(high - offset) // (16 * w)) * 16
                step = -(-(end - first) // (16 * -(-(end - first) // PACK_ROWS[w]))) * 16
                for row in range(first, end, step):
                    blocks.append((t, row, min(step, end - row), parity, h, offset + row * w - begin + MARGIN))
    return blocks


def reduce_kernel(*refs):
    (grads, norms, (g_out, norm_out, flat, land_p, land_d, land_n, land_s),
     (mine, part, first, second, sums, g_buf, ss, ss_all), tiles, (stage, tail),
     (p_send, p_recv, i_send, i_recv, load_sem, g_sem, ss_send, ss_recv, in_sem, out_sem, tail_sem)) = split(refs, (7, 3, 7, 8, 3, 2, 11))
    me, other, dev_x, dev_y, dev_d = neighbours()
    core, x, y = lax.rem(me, 2), lax.rem(me // 2, 2), me // 4
    barrier = pltpu.get_barrier_semaphore()
    for d in range(1, NDEV):
        pl.semaphore_signal(barrier, inc=1, device_id=(lax.rem(me + d, NDEV),), device_id_type=MESH)

    tail[...] = jnp.zeros_like(tail)
    line = 0
    for n in norms:
        for layer in range(n.shape[0]):
            for j in COLUMNS:
                tail[pl.ds(line, 1), :] = n[pl.ds(layer, 1), pl.ds(j * LANES, LANES)].astype(F32)
                line += 1

    def pack(place, chip, quarter):
        blocks = pack_blocks(chip, quarter)

        def load(b):
            t, row, rows = blocks[b][:3]
            return pltpu.make_async_copy(grads[t].at[pl.ds(row, rows)], tiles[width_slot(WIDTHS[t])].at[b % 2, pl.ds(0, rows)], in_sem.at[b % 2])

        def store(b):
            t, _, rows, parity, h, to = blocks[b]
            size = rows * WIDTHS[t]
            return pltpu.make_async_copy(stage.at[b % 2, pl.ds(0, size)], flat.at[place, quarter, parity, h, pl.ds(to, size), 0], out_sem.at[b % 2])

        load(0).start()
        load(1).start()
        tail_copies = [pltpu.make_async_copy(tail, flat.at[place, quarter, quarter, quarter, pl.ds(MARGIN + QUARTER - TAIL, TAIL), 0], tail_sem)
                       for _ in range(chip * quarter // 3)]
        for copy in tail_copies:
            copy.start()
        for b, block in enumerate(blocks):
            t, rows = block[0], block[2]
            w = WIDTHS[t]
            tile = tiles[width_slot(w)]
            group = row_group(rows, w)
            load(b).wait()
            if b >= 2:
                store(b - 2).wait()

            @pl.loop(0, rows // group)
            def _(i):
                for j in range(w):
                    values = tile[b % 2, pl.ds(pl.multiple_of(i * group, 16), group), pl.ds(j * LANES, LANES)].astype(F32)
                    if w == 1:
                        stage[b % 2, pl.ds(pl.multiple_of(i * group, 16), group), :] = values
                    else:
                        stage[b % 2, pl.ds(i * (group * w) + j, group, stride=w), :] = values

            store(b).start()
            if b + 2 < len(blocks):
                load(b + 2).start()
        store(len(blocks) - 2).wait()
        store(len(blocks) - 1).wait()
        for copy in tail_copies:
            copy.wait()

    def place_of(kind, h):
        return ((CHIP_D, CHIP_D), (CHIP_X, CHIP_Y), (CHIP_Y, CHIP_X), (CHIP_OWN, CHIP_OWN))[kind][h]

    def chunk(kind, h, i, parity):
        return flat.at[place_of(kind, h), i // 4, parity, h, pl.ds(MARGIN + RS_ROWS * lax.rem(i, 4), RS_ROWS)]

    def start_row(h, i):
        return RS_HALF_START * h + RS_ROWS * i

    def partner_copy(kind, h, i):
        return pltpu.make_async_remote_copy(
            src_ref=chunk(kind, h, i, 1 - core), dst_ref=land_p.at[kind, h, i],
            send_sem=p_send.at[kind, h, i], recv_sem=p_recv.at[kind, h, i],
            device_id=(me + other,), device_id_type=MESH)

    def link_copy(kind, h, i):
        land = (land_d, land_n, land_s)[kind]
        to = ((dev_x, dev_y), (dev_x, dev_y), (dev_y, dev_x))[kind][h]
        return pltpu.make_async_remote_copy(
            src_ref=sums.at[kind, h, i], dst_ref=land.at[h, i, pl.ds(0, RS_ROWS), 0],
            send_sem=i_send.at[kind, h, i], recv_sem=i_recv.at[kind, h, i],
            device_id=(to,), device_id_type=MESH)

    def load_mine(kind, h, i):
        return pltpu.make_async_copy(chunk(kind, h, i, core).at[:, 0], mine.at[h], load_sem.at[0, h])

    def load_part(kind, h, i):
        return pltpu.make_async_copy(land_p.at[kind, h, i, pl.ds(0, RS_ROWS), 0], part.at[h], load_sem.at[1, h])

    def load_link(land, buf, n, h, i):
        return pltpu.make_async_copy(land.at[h, i, pl.ds(0, RS_ROWS), 0], buf.at[h], load_sem.at[n, h])

    def store_g(h, i):
        return pltpu.make_async_copy(g_buf.at[h], g_out.at[pl.ds(start_row(h, i), RS_ROWS), 0], g_sem.at[h])

    def exchange(kinds, begin, end):
        @pl.loop(begin, end)
        def _(i):
            for kind in kinds:
                for h in HALVES:
                    partner_copy(kind, h, i).start()

    def send(kind, begin, end):
        @pl.loop(begin, end)
        def _(i):
            for h in HALVES:
                load_mine(kind, h, i).start()
            for h in HALVES:
                partner_copy(kind, h, i).wait_recv()
                load_part(kind, h, i).start()
                if kind == KIND_S:
                    link_copy(KIND_D, h, i).wait_recv()
                    load_link(land_d, first, 2, h, i).start()
            for h in HALVES:
                load_mine(kind, h, i).wait()
                load_part(kind, h, i).wait()
                total = mine[h] + part[h]
                if kind == KIND_S:
                    load_link(land_d, first, 2, h, i).wait()
                    total = total + first[h]
                sums[kind, h, i] = total
                link_copy(kind, h, i).start()

    @pl.loop(0, 8)
    def _(unit):
        place, quarter = unit // 2, lax.rem(unit, 2)
        flip_x, flip_y = 1 - place // 2, 1 - lax.rem(place, 2)
        chip = (x + flip_x * (1 - 2 * x)) + 2 * (y + flip_y * (1 - 2 * y))
        for case in range(8):
            @pl.when(2 * chip + quarter == case)
            def _():
                pack(place, case // 2, case % 2)

        @pl.when(unit == 0)
        def _():
            pl.semaphore_wait(barrier, NDEV - 1)

        @pl.when(unit < 2)
        def _():
            exchange((KIND_D,), 4 * quarter, 4 * quarter + 4)
            send(KIND_D, 4 * quarter, 4 * quarter + 4)

    exchange((KIND_N, KIND_S), 0, 8)
    exchange((KIND_O,), 0, 8)
    send(KIND_N, 0, 8)
    send(KIND_S, 0, 8)

    def last(i, acc):
        for h in HALVES:
            load_mine(KIND_O, h, i).start()
            partner_copy(KIND_O, h, i).wait_recv()
            load_part(KIND_O, h, i).start()
        for h in HALVES:
            link_copy(KIND_N, h, i).wait_recv()
            load_link(land_n, first, 2, h, i).start()
        for h in HALVES:
            link_copy(KIND_S, h, i).wait_recv()
            load_link(land_s, second, 3, h, i).start()
            load_mine(KIND_O, h, i).wait()
            load_part(KIND_O, h, i).wait()
            load_link(land_n, first, 2, h, i).wait()
            load_link(land_s, second, 3, h, i).wait()

            @pl.when(i > 0)
            def _():
                store_g(h, i - 1).wait()

            g = ((mine[h] + part[h]) + (first[h] + second[h])) * (1.0 / NDEV)
            g_buf[h] = g
            store_g(h, i).start()
            square = g * g
            if h == 1:
                row = lax.broadcasted_iota(jnp.int32, (RS_ROWS, LANES), 0) + RS_ROWS * i
                square = jnp.where(row >= 8 * RS_ROWS - RS_HALF_START, square, 0.0)
            acc = acc + jnp.sum(square, axis=0, keepdims=True)
        return acc

    acc = lax.fori_loop(0, 8, last, jnp.zeros((1, LANES), F32))
    ss[...] = jnp.broadcast_to(acc, (8, LANES))
    for h in HALVES:
        store_g(h, 7).wait()

    @pl.loop(0, 8)
    def _(i):
        for h in HALVES:
            for kind in range(4):
                partner_copy(kind, h, i).wait_send()
            for kind in range(3):
                link_copy(kind, h, i).wait_send()

    def norm_copy(d):
        return pltpu.make_async_remote_copy(
            src_ref=ss, dst_ref=ss_all.at[d], send_sem=ss_send.at[d], recv_sem=ss_recv.at[d],
            device_id=(lax.rem(me + d, NDEV),), device_id_type=MESH)

    for d in range(1, NDEV):
        norm_copy(d).start()
    ss_all[0] = ss[...]
    for d in range(1, NDEV):
        norm_copy(d).wait()
    total = jnp.zeros((8, LANES), F32)
    for dev in range(NDEV):
        total = total + ss_all[lax.rem(me - dev + NDEV, NDEV)]
    norm_out[...] = jnp.broadcast_to(jnp.sqrt(jnp.sum(total, axis=1, keepdims=True)), (8, LANES))


def reduce_grads(grads, norms):
    land = jax.ShapeDtypeStruct((2, 8, RS_ROWS, 1, LANES), F32)
    land_p = jax.ShapeDtypeStruct((4, 2, 8, RS_ROWS, 1, LANES), F32)
    flat = jax.ShapeDtypeStruct((4, 2, 2, 2, QUARTER + 2 * MARGIN, 1, LANES), F32)
    buf = pltpu.VMEM((2, RS_ROWS, LANES), F32)
    partner, link, pair, all_devs = DMA((4, 2, 8)), DMA((3, 2, 8)), DMA((2,)), DMA((NDEV,))
    outs = pl.pallas_call(
        reduce_kernel,
        name="reduce_grads",
        out_shape=[jax.ShapeDtypeStruct((SEG, 1, LANES), F32), jax.ShapeDtypeStruct((8, LANES), F32), flat, land_p, land, land, land],
        in_specs=[ANY] * 7 + [VMEM_SPEC] * 3,
        out_specs=[ANY, VMEM_SPEC] + [ANY] * 5,
        scratch_shapes=[buf] * 4 + [pltpu.VMEM((3, 2, 8, RS_ROWS, LANES), F32), buf, pltpu.VMEM((8, LANES), F32), pltpu.VMEM((NDEV, 8, LANES), F32)]
        + tile_scratch(2, PACK_ROWS.values()) + [pltpu.VMEM((2, PACK_STAGE, LANES), F32), pltpu.VMEM((TAIL, LANES), F32)]
        + [partner, partner, link, link, DMA((4, 2)), pair, all_devs, all_devs, pair, pair, DMA],
        compiler_params=pltpu.CompilerParams(collective_id=0, has_side_effects=True, vmem_limit_bytes=VMEM_LIMIT),
        cost_estimate=COST,
    )(*grads, *norms)
    return outs[0], outs[1]


def adam_rows(g, m, v, p, norm_row, lr, decay):
    clip = jnp.minimum(1.0, MAX_NORM / (norm_row + CLIP_EPS))
    clipped = clip * g
    new_m = BETA_ONE * m + (1.0 - BETA_ONE) * clipped
    new_v = BETA_TWO * v + (1.0 - BETA_TWO) * clipped * clipped
    adam_dir = (new_m / BIAS_ONE) / (jnp.sqrt(new_v / BIAS_TWO) + ADAM_EPS)
    decay_term = jnp.where(decay, WEIGHT_DECAY * p, 0.0)
    return p - lr * (decay_term + adam_dir), new_m, new_v


UP_ROWS = 1824
UP_LAST = SEG - 15 * UP_ROWS
SUB = 152


def decay_rows(me, start, rows):
    return lax.broadcasted_iota(jnp.int32, (rows, LANES), 0) + (SEG * me + start) < MATRIX_ROWS


def gather_kernel(g, m, v, p, norm, lr, full, late, gb, mb, vb, pb, new_p, late_p,
                  load_sem, own_sem, late_sem, own_send, own_recv, fwd_send, fwd_recv, p_send, p_recv):
    me, other, dev_x, dev_y, dev_d = neighbours()
    partner = me + other
    barrier = pltpu.get_barrier_semaphore()
    for dev in (partner, dev_x, dev_y):
        pl.semaphore_signal(barrier, inc=1, device_id=(dev,), device_id_type=MESH)
    pl.semaphore_wait(barrier, 3)
    to = (dev_x, dev_y, partner)
    sources = (me, dev_x, dev_y, dev_d)

    def is_last(h, i):
        return h == 1 and isinstance(i, int) and i == HALF - 1

    def start_row(h, i):
        return PIECE * (PIECES - 1) if is_last(h, i) else PIECE * (HALF * h + i)

    def size(h, i):
        return PIECE_LAST if is_last(h, i) else PIECE

    def rows_of(dev, h, i):
        return full.at[pl.ds(SEG * dev + start_row(h, i), size(h, i)), 0]

    def loads(h, i):
        return loads_at(h, start_row(h, i), size(h, i))

    def loads_at(h, start, rows):
        start = pl.multiple_of(start, 8)
        copies = [pltpu.make_async_copy(g.at[pl.ds(start, rows), 0], gb.at[h, pl.ds(0, rows)], load_sem.at[0, h])]
        for n, (src, buf) in enumerate(((m, mb), (v, vb), (p, pb))):
            copies.append(pltpu.make_async_copy(src.at[pl.ds(start, rows)], buf.at[h, pl.ds(0, rows)], load_sem.at[n + 1, h]))
        return copies

    def own_copy(n, h, i):
        return pltpu.make_async_remote_copy(
            src_ref=new_p.at[h, i, pl.ds(0, size(h, i))], dst_ref=rows_of(me, h, i),
            send_sem=own_send.at[n, h, i], recv_sem=own_recv.at[n, h, i], device_id=(to[n],), device_id_type=MESH)

    def own_store(h, i):
        return pltpu.make_async_copy(new_p.at[h, i, pl.ds(0, size(h, i))], rows_of(me, h, i), own_sem.at[h, i])

    def forward(h, i):
        src = rows_of((dev_y, dev_x)[h], h, i)
        return pltpu.make_async_remote_copy(
            src_ref=src, dst_ref=src, send_sem=fwd_send.at[h, i], recv_sem=fwd_recv.at[h, i],
            device_id=((dev_x, dev_y)[h],), device_id_type=MESH)

    def arrival(n, h, i):
        src = rows_of((dev_x, dev_y, partner)[n], h, i)
        return pltpu.make_async_remote_copy(
            src_ref=src, dst_ref=src, send_sem=own_send.at[n, h, i], recv_sem=own_recv.at[n, h, i],
            device_id=(to[n],), device_id_type=MESH)

    def forward_arrival(h, i):
        src = rows_of(dev_d, h, i)
        return pltpu.make_async_remote_copy(
            src_ref=src, dst_ref=src, send_sem=fwd_send.at[h, i], recv_sem=fwd_recv.at[h, i],
            device_id=((dev_x, dev_y)[h],), device_id_type=MESH)

    def partner_copy(q, h, i):
        src = rows_of(sources[q], h, i)
        return pltpu.make_async_remote_copy(
            src_ref=src, dst_ref=src, send_sem=p_send.at[q - 1, h, i], recv_sem=p_recv.at[q - 1, h, i],
            device_id=(partner,), device_id_type=MESH)

    def partner_arrival(q, h, i):
        src = rows_of(sources[q] + other, h, i)
        return pltpu.make_async_remote_copy(
            src_ref=src, dst_ref=src, send_sem=p_send.at[q - 1, h, i], recv_sem=p_recv.at[q - 1, h, i],
            device_id=(partner,), device_id_type=MESH)

    def each(body):
        @pl.loop(0, HALF - 1)
        def _(i):
            body(i)

        body(HALF - 1)

    norm_row = norm[0:1, :]
    for h in HALVES:
        for copy in loads(h, 0):
            copy.start()

    def compute(h, out, first):
        @pl.loop(0, PIECE // SUB)
        def _(s):
            start = pl.multiple_of(s * SUB, 8)
            sub = pl.ds(start, SUB)
            out[sub] = adam_rows(gb[h, sub], mb[h, sub], vb[h, sub], pb[h, sub], norm_row, lr[0], decay_rows(me, first + start, SUB))[0]

    def update(i):
        for h in HALVES:
            for copy in loads(h, i):
                copy.wait()

            compute(h, new_p.at[h, i], start_row(h, i))
            for n in ((1, 0, 2) if h == 0 else (0, 1, 2)):
                own_copy(n, h, i).start()
            own_store(h, i).start()
            if isinstance(i, int):
                continue
            for last in (False, True):
                @pl.when((i == HALF - 2) == last)
                def _():
                    for copy in loads(h, HALF - 1 if last else i + 1):
                        copy.start()

    each(update)

    def late_store(src, to, n):
        return pltpu.make_async_copy(src, late.at[pl.ds(to, src.shape[0]), 0], late_sem.at[n])

    def late_piece(j):
        return late_store(late_p.at[j], 8 + PIECE * j, j)

    edges = [late_store(new_p.at[1, HALF - 2, pl.ds(PIECE - 8, 8)], 0, 6),
             late_store(new_p.at[1, HALF - 1, pl.ds(0, 8)], LATE_ROWS - 8, 7)]
    for copy in edges:
        copy.start()

    @pl.loop(0, LATE_END - LATE_FIRST)
    def _(j):
        first = PIECE * (LATE_FIRST + j)
        for copy in loads_at(0, first, PIECE):
            copy.start()
        for copy in loads_at(0, first, PIECE):
            copy.wait()
        compute(0, late_p.at[j], first)
        late_piece(j).start()

    def pass_on(i):
        arrival(1, 0, i).wait_recv()
        forward(0, i).start()
        partner_copy(2, 0, i).start()
        arrival(0, 1, i).wait_recv()
        forward(1, i).start()
        partner_copy(1, 1, i).start()
        arrival(0, 0, i).wait_recv()
        partner_copy(1, 0, i).start()
        arrival(1, 1, i).wait_recv()
        partner_copy(2, 1, i).start()

    each(pass_on)

    def pass_last(i):
        for h in HALVES:
            forward_arrival(h, i).wait_recv()
            partner_copy(3, h, i).start()

    each(pass_last)

    def finish(i):
        for h in HALVES:
            own_store(h, i).wait()
            arrival(2, h, i).wait_recv()
            for n in range(3):
                own_copy(n, h, i).wait_send()
            forward(h, i).wait_send()
            for q in range(1, 4):
                partner_copy(q, h, i).wait_send()
                partner_arrival(q, h, i).wait_recv()

    each(finish)
    for copy in edges:
        copy.wait()

    @pl.loop(0, LATE_END - LATE_FIRST)
    def _(j):
        late_piece(j).wait()


def gather_params(g, m, v, p, norm, lr):
    buf = pltpu.VMEM((2, PIECE, LANES), F32)
    pairs = DMA((2, HALF))
    triples = DMA((3, 2, HALF))
    return pl.pallas_call(
        gather_kernel,
        name="gather_params",
        out_shape=[jax.ShapeDtypeStruct((FLAT_ROWS, 1, LANES), F32), jax.ShapeDtypeStruct((LATE_ROWS, 1, LANES), F32)],
        in_specs=[ANY] * 4 + [VMEM_SPEC, SMEM_SPEC],
        out_specs=[ANY, ANY],
        scratch_shapes=[buf, buf, buf, buf, pltpu.VMEM((2, HALF, PIECE, LANES), F32), pltpu.VMEM((LATE_END - LATE_FIRST, PIECE, LANES), F32),
                        DMA((4, 2)), pairs, DMA((8,)), triples, triples, pairs, pairs, triples, triples],
        compiler_params=pltpu.CompilerParams(collective_id=1, has_side_effects=True, vmem_limit_bytes=VMEM_LIMIT),
        cost_estimate=COST,
    )(g, m, v, p, norm, lr)


def state_kernel(g, m, v, p, norm, lr, new_p, new_m, new_v, gb, g_sem):
    me = lax.axis_index("dp")
    i = pl.program_id(0)

    def load(j, last):
        rows = UP_LAST if last else UP_ROWS
        return pltpu.make_async_copy(g.at[pl.ds(j * UP_ROWS, rows), 0], gb.at[lax.rem(j, 2), pl.ds(0, rows)], g_sem.at[lax.rem(j, 2)])

    @pl.when(i == 0)
    def _():
        load(i, False).start()

    @pl.when(i < 14)
    def _():
        load(i + 1, False).start()

    @pl.when(i == 14)
    def _():
        load(i + 1, True).start()

    @pl.when(i < 15)
    def _():
        load(i, False).wait()

    @pl.when(i == 15)
    def _():
        load(i, True).wait()

    norm_row = norm[0:1, :]

    @pl.loop(0, UP_ROWS // SUB)
    def _(s):
        start = pl.multiple_of(s * SUB, 8)
        rows = pl.ds(start, SUB)
        new_p[rows], new_m[rows], new_v[rows] = adam_rows(
            gb[lax.rem(i, 2), rows], m[rows], v[rows], p[rows], norm_row, lr[0], decay_rows(me, i * UP_ROWS + start, SUB))


def new_state(g, m, v, p, norm, lr):
    block = pl.BlockSpec((UP_ROWS, LANES), lambda i: (i, 0))
    return pl.pallas_call(
        state_kernel,
        name="new_state",
        grid=(16,),
        out_shape=[jax.ShapeDtypeStruct((SEG, LANES), F32)] * 3,
        in_specs=[ANY, block, block, block, pl.BlockSpec((8, LANES), lambda i: (0, 0)), SMEM_SPEC],
        out_specs=[block] * 3,
        scratch_shapes=[pltpu.VMEM((2, UP_ROWS, LANES), F32), DMA((2,))],
        compiler_params=pltpu.CompilerParams(vmem_limit_bytes=VMEM_LIMIT),
        cost_estimate=COST,
    )(g, m, v, p, norm, lr)


def solution(mesh):
    def local_step(*arrays):
        grads = [a.reshape(r, w * LANES) for a, r, w in zip(arrays[:7], NAMES_ROWS, WIDTHS)]
        norms = [a.reshape(s) for a, s in zip(arrays[7:10], GAINS)]
        master, exp_avg, exp_avg_sq = [a.reshape(SEG, LANES) for a in arrays[10:13]]
        lr = arrays[13].reshape(1)
        g, norm = reduce_grads(grads, norms)
        full, late = gather_params(g, exp_avg, exp_avg_sq, master, norm, lr)
        late = lax.all_gather(late, "dp", tiled=True)
        state = new_state(g, exp_avg, exp_avg_sq, master, norm, lr)
        params = unpack_late(full, late, unpack_early(full))
        shapes = SHAPES + GAINS[:2] + [(D,)]
        return tuple([a.reshape(-1) for a in state] + [a.reshape(s) for a, s in zip(params, shapes)] + [norm[0, 0]])

    return jax.shard_map(local_step, mesh=mesh, in_specs=(P("dp"),) * 13 + (P(),), out_specs=(P("dp"),) * 3 + (P(),) * 11, check_vma=False)
```

time: 1190 us -> 1050 us (0.88)
  Pallas kernels: 1170 us -> 1010 us
  waiting for transfers between devices: 0 us -> 16 us
  between operations: 1.37 us -> 14.7 us
  local copies, waits for them, and re-layouts: 14.3 us -> 1.18 us
    pallas_call x3, Pallas kernels: 626 us -> 461 us  [the longest x1 401 us: gather_params(): pl.pallas_call(gather_kernel, name='gather_params', out_shape=[jax.ShapeD...]
    all_gather x0 -> x1, waiting for transfers between devices: none -> 16 us  [local_step(): late = lax.all_gather(late, 'dp', tiled=True)]
    unnamed x20 -> x0, local copies, waits for them, and re-layouts: 13.8 us -> none
  transfers between devices with their start and end apart: 0 -> 1, of which waited for: 0 -> 1; matrix products, arithmetic and copies ran while one was open for 0% -> 0% of each run, Pallas kernels for 0% -> 9%
where the time goes in v2:
time: 1050 us
  Pallas kernels  1010 us (96%)
  waiting for transfers between devices  16 us (2%)
  between operations  14.7 us (1%)
    pallas_call x1, Pallas kernels, reduce_grads(): pl.pallas_call(reduce_kernel, name='reduce_grads', out_shape=[jax.ShapeDt...  511 us
    pallas_call x1, Pallas kernels, gather_params(): pl.pallas_call(gather_kernel, name='gather_params', out_shape=[jax.ShapeD...  401 us
    pallas_call x1, Pallas kernels, unpack_early(): pl.pallas_call(unpack_early_kernel, name='unpack_early', out_shape=TENSOR...  47.2 us
    pallas_call x1, Pallas kernels, new_state(): pl.pallas_call(state_kernel, name='new_state', grid=(16,), out_shape=[jax...  42.8 us
  transfers between devices with their start and end apart: 1, of which 1 were waited for; matrix products, arithmetic and copies ran while one was open for 0% of the time, Pallas kernels for 9%

profile of v2, /device:TPU:0, one launch (start us, length us, event | category | flops | bytes accessed | tf_op | source)
XLA Modules:
  0.0 1047.8 jit_solution(6760001863550097613)
XLA Ops:
  7.2 0.0 all-gather.2.cloned.1.call-start
  7.9 511.0 %reduce_grads.1 = (f32[29125,1,128]{2,1,0:T(1,128)}, f32[8,128]{1,0:T(8,128)}, f32[4,2,2,2,8500,1,128]{6,5,4,3,2,1,0:T(1,128)}, f32[4,2,8,1821,1,128]{5,4,3,2,1,...) custom-call(bf16[1792,896]{1,0:T(8,128)(2,1)} %bitcast.38, ...), custom_call_target="tpu_custom_call" | custom-call | flops 200000000 | bytes 100000000 | tf_op jit(solution)/shard_map/reduce_grads/pallas_call | solution.py:463
  518.9 400.7 %gather_params.1 = (f32[233000,1,128]{2,1,0:T(1,128)}, f32[5488,1,128]{2,1,0:T(1,128)}) custom-call(f32[29125,1,128]{2,1,0:T(1,128)} %get-tuple-element.35.g, f32[29125,128]{1,0:T(8,128)} %bitcast.26, f32[29125,128]{1,0:T(8,128)} %bitcast.28, f32[29125,128]{1,0:T(8,128)} %bitcast.30, f32[8,128]{1,0:T(8,128)} %get-tuple-element.36.norm, f32[1]{0:T(128)} %bitcast.25.lr), custom_call_target="tpu_custom_call" | custom-call | flops 200000000 | bytes 100000000 | tf_op jit(solution)/shard_map/gather_params/pallas_call | solution.py:672
  919.6 0.0 all-gather.2.cloned.1.call-update
  919.6 1.2 slice.3
  920.8 47.2 %unpack_early.1 = (bf16[1792,896]{1,0:T(8,128)(2,1)}, bf16[1792,128]{1,0:T(8,128)(2,1)}, bf16[1792,128]{1,0:T(8,128)(2,1)}, bf16[1792,896]{1,0:T(8,128)(2,1)}, b...) custom-call(f32[233000,1,128]{2,1,0:T(1,128)} %get-tuple-element.40.flat), custom_call_target="tpu_custom_call" | custom-call | flops 200000000 | bytes 100000000 | tf_op jit(solution)/shard_map/unpack_early/pallas_call | solution.py:174
  967.9 1.3 reduce
  969.2 42.8 %new_state.1 = (f32[29125,128]{1,0:T(8,128)}, f32[29125,128]{1,0:T(8,128)}, f32[29125,128]{1,0:T(8,128)}) custom-call(f32[29125,1,128]{2,1,0:T(1,128)} %get-tuple-element.35.g, f32[29125,128]{1,0:T(8,128)} %bitcast.27, f32[29125,128]{1,0:T(8,128)} %bitcast.29, f32[29125,128]{1,0:T(8,128)} %bitcast.31, f32[8,128]{1,0:T(8,128)} %get-tuple-element.36.norm, ...), custom_call_target="tpu_custom_call" | custom-call | flops 200000000 | bytes 100000000 | tf_op jit(solution)/shard_map/new_state/pallas_call | solution.py:725
  1012.0 16.0 %all-gather.2.cloned.1.call-done.late = f32[43904,1,128]{2,1,0:T(1,128)} async-done(((f32[5488,1,128]{2,1,0:T(1,128)}), f32[43904,1,128]{2,1,0:T(1,128)}) %all-gather.2.cloned.1.call-update) | async-done | bytes 22478864 | tf_op jit(solution)/shard_map/all_gather | solution.py:746
  1028.0 12.9 %unpack_late.1 = (bf16[1792,896]{1,0:T(8,128)(2,1)}, bf16[1792,4864]{1,0:T(8,128)(2,1)}, bf16[1792,4864]{1,0:T(8,128)(2,1)}, bf16[9728,896]{1,0:T(8,128)(2,1)}) custom-call(f32[233000,1,128]{2,1,0:T(1,128)} %get-tuple-element.40.flat, ...), custom_call_target="tpu_custom_call", output_to_operand_aliasing={{0}: (2, {}), {1}: (3, {}), {2}: (4, {}), {3}: (5, {})} | custom-call | flops 200000000 | bytes 100000000 | tf_op jit(solution)/shard_map/unpack_late/pallas_call | solution.py:196
Async XLA Ops:
  7.2 1020.8 %all-gather.2.cloned.1.call-start = ((), (), s32[]{:S(2)}) async-start(), calls=%async_computation | async-start | bytes 25288704 | tf_op jit(solution)/shard_map/all_gather | solution.py:746
Sparse Core Ops, SparseCore 0:
  919.7 108.2 all-gather.1

commit v3 on v2

--- a/solution.py
+++ b/solution.py
@@ -218,24 +218,27 @@
     return me, other, me + step_x, me + step_y, me + step_x + step_y
 
 
-RS_ROWS = 1821
-RS_HALF_START = SEG - 8 * RS_ROWS
+CHUNKS = 16
+RS_ROWS = 911
+RS_HALF_START = SEG - CHUNKS * RS_ROWS
+UNITS = CHUNKS // 4
 KIND_D, KIND_N, KIND_S, KIND_O = range(4)
 CHIP_D, CHIP_X, CHIP_Y, CHIP_OWN = range(4)
-QUARTER = 4 * RS_ROWS
+UNIT_ROWS = 4 * RS_ROWS
 MARGIN = 16 * 38
 PACK_ROWS = {38: 112, 7: 608, 1: 896}
 PACK_STAGE = 112 * 38
-
-
-def pack_blocks(chip, quarter):
+PACK_SLOTS = 3
+
+
+def pack_blocks(chip, unit):
     blocks = []
     for parity in HALVES:
         for h in HALVES:
-            begin = SEG * (2 * chip + parity) + RS_HALF_START * h + QUARTER * quarter
+            begin = SEG * (2 * chip + parity) + RS_HALF_START * h + UNIT_ROWS * unit
             for t in TENSORS:
                 w, offset, total = WIDTHS[t], OFFSETS[t], NAMES_ROWS[t]
-                low, high = max(begin, offset), min(begin + QUARTER, offset + total * w)
+                low, high = max(begin, offset), min(begin + UNIT_ROWS, offset + total * w)
                 if low >= high:
                     continue
                 first = (low - offset) // (16 * w) * 16
@@ -264,22 +267,22 @@
                 tail[pl.ds(line, 1), :] = n[pl.ds(layer, 1), pl.ds(j * LANES, LANES)].astype(F32)
                 line += 1
 
-    def pack(place, chip, quarter):
-        blocks = pack_blocks(chip, quarter)
+    def pack(place, chip, unit):
+        blocks = pack_blocks(chip, unit)
 
         def load(b):
             t, row, rows = blocks[b][:3]
-            return pltpu.make_async_copy(grads[t].at[pl.ds(row, rows)], tiles[width_slot(WIDTHS[t])].at[b % 2, pl.ds(0, rows)], in_sem.at[b % 2])
+            return pltpu.make_async_copy(grads[t].at[pl.ds(row, rows)], tiles[width_slot(WIDTHS[t])].at[b % PACK_SLOTS, pl.ds(0, rows)], in_sem.at[b % PACK_SLOTS])
 
         def store(b):
             t, _, rows, parity, h, to = blocks[b]
             size = rows * WIDTHS[t]
-            return pltpu.make_async_copy(stage.at[b % 2, pl.ds(0, size)], flat.at[place, quarter, parity, h, pl.ds(to, size), 0], out_sem.at[b % 2])
-
-        load(0).start()
-        load(1).start()
-        tail_copies = [pltpu.make_async_copy(tail, flat.at[place, quarter, quarter, quarter, pl.ds(MARGIN + QUARTER - TAIL, TAIL), 0], tail_sem)
-                       for _ in range(chip * quarter // 3)]
+            return pltpu.make_async_copy(stage.at[b % PACK_SLOTS, pl.ds(0, size)], flat.at[place, unit, parity, h, pl.ds(to, size), 0], out_sem.at[b % PACK_SLOTS])
+
+        for b in range(PACK_SLOTS):
+            load(b).start()
+        tail_copies = [pltpu.make_async_copy(tail, flat.at[place, unit, 1, 1, pl.ds(MARGIN + UNIT_ROWS - TAIL, TAIL), 0], tail_sem)
+                       for _ in range(chip * unit // (3 * UNITS - 3))]
         for copy in tail_copies:
             copy.start()
         for b, block in enumerate(blocks):
@@ -288,23 +291,23 @@
             tile = tiles[width_slot(w)]
             group = row_group(rows, w)
             load(b).wait()
-            if b >= 2:
-                store(b - 2).wait()
+            if b >= PACK_SLOTS:
+                store(b - PACK_SLOTS).wait()
 
             @pl.loop(0, rows // group)
             def _(i):
                 for j in range(w):
-                    values = tile[b % 2, pl.ds(pl.multiple_of(i * group, 16), group), pl.ds(j * LANES, LANES)].astype(F32)
+                    values = tile[b % PACK_SLOTS, pl.ds(pl.multiple_of(i * group, 16), group), pl.ds(j * LANES, LANES)].astype(F32)
                     if w == 1:
-                        stage[b % 2, pl.ds(pl.multiple_of(i * group, 16), group), :] = values
+                        stage[b % PACK_SLOTS, pl.ds(pl.multiple_of(i * group, 16), group), :] = values
                     else:
-                        stage[b % 2, pl.ds(i * (group * w) + j, group, stride=w), :] = values
+                        stage[b % PACK_SLOTS, pl.ds(i * (group * w) + j, group, stride=w), :] = values
 
             store(b).start()
-            if b + 2 < len(blocks):
-                load(b + 2).start()
-        store(len(blocks) - 2).wait()
-        store(len(blocks) - 1).wait()
+            if b + PACK_SLOTS < len(blocks):
+                load(b + PACK_SLOTS).start()
+        for b in range(len(blocks) - PACK_SLOTS, len(blocks)):
+            store(b).wait()
         for copy in tail_copies:
             copy.wait()
 
@@ -371,29 +374,32 @@
                 sums[kind, h, i] = total
                 link_copy(kind, h, i).start()
 
-    @pl.loop(0, 8)
-    def _(unit):
-        place, quarter = unit // 2, lax.rem(unit, 2)
+    @pl.loop(0, 4 * UNITS)
+    def _(n):
+        place, unit = n // UNITS, lax.rem(n, UNITS)
         flip_x, flip_y = 1 - place // 2, 1 - lax.rem(place, 2)
         chip = (x + flip_x * (1 - 2 * x)) + 2 * (y + flip_y * (1 - 2 * y))
-        for case in range(8):
-            @pl.when(2 * chip + quarter == case)
+        for case in range(4 * UNITS):
+            @pl.when(UNITS * chip + unit == case)
             def _():
-                pack(place, case // 2, case % 2)
-
-        @pl.when(unit == 0)
+                pack(place, case // UNITS, case % UNITS)
+
+        @pl.when(n == 0)
         def _():
             pl.semaphore_wait(barrier, NDEV - 1)
 
-        @pl.when(unit < 2)
+        @pl.when(n < UNITS)
         def _():
-            exchange((KIND_D,), 4 * quarter, 4 * quarter + 4)
-            send(KIND_D, 4 * quarter, 4 * quarter + 4)
-
-    exchange((KIND_N, KIND_S), 0, 8)
-    exchange((KIND_O,), 0, 8)
-    send(KIND_N, 0, 8)
-    send(KIND_S, 0, 8)
+            exchange((KIND_D,), 4 * unit, 4 * unit + 4)
+            send(KIND_D, 4 * unit, 4 * unit + 4)
+
+        @pl.when(n == 3 * UNITS - 1)
+        def _():
+            exchange((KIND_N, KIND_S), 0, CHUNKS)
+            send(KIND_N, 0, CHUNKS)
+
+    exchange((KIND_O,), 0, CHUNKS)
+    send(KIND_S, 0, CHUNKS)
 
     def last(i, acc):
         for h in HALVES:
@@ -421,16 +427,14 @@
             square = g * g
             if h == 1:
                 row = lax.broadcasted_iota(jnp.int32, (RS_ROWS, LANES), 0) + RS_ROWS * i
-                square = jnp.where(row >= 8 * RS_ROWS - RS_HALF_START, square, 0.0)
+                square = jnp.where(row >= CHUNKS * RS_ROWS - RS_HALF_START, square, 0.0)
             acc = acc + jnp.sum(square, axis=0, keepdims=True)
         return acc
 
-    acc = lax.fori_loop(0, 8, last, jnp.zeros((1, LANES), F32))
+    acc = lax.fori_loop(0, CHUNKS, last, jnp.zeros((1, LANES), F32))
     ss[...] = jnp.broadcast_to(acc, (8, LANES))
-    for h in HALVES:
-        store_g(h, 7).wait()
-
-    @pl.loop(0, 8)
+
+    @pl.loop(0, CHUNKS)
     def _(i):
         for h in HALVES:
             for kind in range(4):
@@ -445,6 +449,8 @@
 
     for d in range(1, NDEV):
         norm_copy(d).start()
+    for h in HALVES:
+        store_g(h, CHUNKS - 1).wait()
     ss_all[0] = ss[...]
     for d in range(1, NDEV):
         norm_copy(d).wait()
@@ -455,20 +461,20 @@
 
 
 def reduce_grads(grads, norms):
-    land = jax.ShapeDtypeStruct((2, 8, RS_ROWS, 1, LANES), F32)
-    land_p = jax.ShapeDtypeStruct((4, 2, 8, RS_ROWS, 1, LANES), F32)
-    flat = jax.ShapeDtypeStruct((4, 2, 2, 2, QUARTER + 2 * MARGIN, 1, LANES), F32)
+    land = jax.ShapeDtypeStruct((2, CHUNKS, RS_ROWS, 1, LANES), F32)
+    land_p = jax.ShapeDtypeStruct((4, 2, CHUNKS, RS_ROWS, 1, LANES), F32)
+    flat = jax.ShapeDtypeStruct((4, UNITS, 2, 2, UNIT_ROWS + 2 * MARGIN, 1, LANES), F32)
     buf = pltpu.VMEM((2, RS_ROWS, LANES), F32)
-    partner, link, pair, all_devs = DMA((4, 2, 8)), DMA((3, 2, 8)), DMA((2,)), DMA((NDEV,))
+    partner, link, pair, all_devs, slots = DMA((4, 2, CHUNKS)), DMA((3, 2, CHUNKS)), DMA((2,)), DMA((NDEV,)), DMA((PACK_SLOTS,))
     outs = pl.pallas_call(
         reduce_kernel,
         name="reduce_grads",
         out_shape=[jax.ShapeDtypeStruct((SEG, 1, LANES), F32), jax.ShapeDtypeStruct((8, LANES), F32), flat, land_p, land, land, land],
         in_specs=[ANY] * 7 + [VMEM_SPEC] * 3,
         out_specs=[ANY, VMEM_SPEC] + [ANY] * 5,
-        scratch_shapes=[buf] * 4 + [pltpu.VMEM((3, 2, 8, RS_ROWS, LANES), F32), buf, pltpu.VMEM((8, LANES), F32), pltpu.VMEM((NDEV, 8, LANES), F32)]
-        + tile_scratch(2, PACK_ROWS.values()) + [pltpu.VMEM((2, PACK_STAGE, LANES), F32), pltpu.VMEM((TAIL, LANES), F32)]
-        + [partner, partner, link, link, DMA((4, 2)), pair, all_devs, all_devs, pair, pair, DMA],
+        scratch_shapes=[buf] * 4 + [pltpu.VMEM((3, 2, CHUNKS, RS_ROWS, LANES), F32), buf, pltpu.VMEM((8, LANES), F32), pltpu.VMEM((NDEV, 8, LANES), F32)]
+        + tile_scratch(PACK_SLOTS, PACK_ROWS.values()) + [pltpu.VMEM((PACK_SLOTS, PACK_STAGE, LANES), F32), pltpu.VMEM((TAIL, LANES), F32)]
+        + [partner, partner, link, link, DMA((4, 2)), pair, all_devs, all_devs, slots, slots, DMA],
         compiler_params=pltpu.CompilerParams(collective_id=0, has_side_effects=True, vmem_limit_bytes=VMEM_LIMIT),
         cost_estimate=COST,
     )(*grads, *norms)
@@ -480,7 +486,7 @@
     clipped = clip * g
     new_m = BETA_ONE * m + (1.0 - BETA_ONE) * clipped
     new_v = BETA_TWO * v + (1.0 - BETA_TWO) * clipped * clipped
-    adam_dir = (new_m / BIAS_ONE) / (jnp.sqrt(new_v / BIAS_TWO) + ADAM_EPS)
+    adam_dir = (new_m * (1.0 / BIAS_ONE)) / (jnp.sqrt(new_v * (1.0 / BIAS_TWO)) + ADAM_EPS)
     decay_term = jnp.where(decay, WEIGHT_DECAY * p, 0.0)
     return p - lr * (decay_term + adam_dir), new_m, new_v
 
@@ -501,7 +507,6 @@
     barrier = pltpu.get_barrier_semaphore()
     for dev in (partner, dev_x, dev_y):
         pl.semaphore_signal(barrier, inc=1, device_id=(dev,), device_id_type=MESH)
-    pl.semaphore_wait(barrier, 3)
     to = (dev_x, dev_y, partner)
     sources = (me, dev_x, dev_y, dev_d)
 
@@ -576,6 +581,7 @@
     for h in HALVES:
         for copy in loads(h, 0):
             copy.start()
+    pl.semaphore_wait(barrier, 3)
 
     def compute(h, out, first):
         @pl.loop(0, PIECE // SUB)

time: 1050 us -> 1050 us (level)
  no operation moved by 1% of the time
where the time goes in v3:
time: 1050 us; the launch traced here: 1040 us
  Pallas kernels  1010 us (96%)
  waiting for transfers between devices  17 us (2%)
  between operations  14.7 us (1%)
    pallas_call x1, Pallas kernels, reduce_grads(): pl.pallas_call(reduce_kernel, name='reduce_grads', out_shape=[jax.ShapeDt...  505 us
    pallas_call x1, Pallas kernels, gather_params(): pl.pallas_call(gather_kernel, name='gather_params', out_shape=[jax.ShapeD...  399 us
    pallas_call x1, Pallas kernels, unpack_early(): pl.pallas_call(unpack_early_kernel, name='unpack_early', out_shape=TENSOR...  47.2 us
    pallas_call x1, Pallas kernels, new_state(): pl.pallas_call(state_kernel, name='new_state', grid=(16,), out_shape=[jax...  42.8 us
  transfers between devices with their start and end apart: 1, of which 1 were waited for; matrix products, arithmetic and copies ran while one was open for 0% of the time, Pallas kernels for 9%

profile of v3, /device:TPU:0, one launch (start us, length us, event | category | flops | bytes accessed | tf_op | source)
XLA Modules:
  0.0 1041.9 jit_solution(8167357878652235924)
XLA Ops:
  7.2 0.0 all-gather.2.cloned.1.call-start
  7.9 505.5 %reduce_grads.1 = (f32[29125,1,128]{2,1,0:T(1,128)}, f32[8,128]{1,0:T(8,128)}, f32[4,4,2,2,4860,1,128]{6,5,4,3,2,1,0:T(1,128)}, f32[4,2,16,911,1,128]{5,4,3,2,1,...) custom-call(bf16[1792,896]{1,0:T(8,128)(2,1)} %bitcast.38, ...), custom_call_target="tpu_custom_call" | custom-call | flops 200000000 | bytes 100000000 | tf_op jit(solution)/shard_map/reduce_grads/pallas_call | solution.py:469
  513.4 399.3 %gather_params.1 = (f32[233000,1,128]{2,1,0:T(1,128)}, f32[5488,1,128]{2,1,0:T(1,128)}) custom-call(f32[29125,1,128]{2,1,0:T(1,128)} %get-tuple-element.35.g, f32[29125,128]{1,0:T(8,128)} %bitcast.26, f32[29125,128]{1,0:T(8,128)} %bitcast.28, f32[29125,128]{1,0:T(8,128)} %bitcast.30, f32[8,128]{1,0:T(8,128)} %get-tuple-element.36.norm, f32[1]{0:T(128)} %bitcast.25.lr), custom_call_target="tpu_custom_call" | custom-call | flops 200000000 | bytes 100000000 | tf_op jit(solution)/shard_map/gather_params/pallas_call | solution.py:678
  912.6 0.0 all-gather.2.cloned.1.call-update
  912.7 1.2 slice.3
  913.9 47.2 %unpack_early.1 = (bf16[1792,896]{1,0:T(8,128)(2,1)}, bf16[1792,128]{1,0:T(8,128)(2,1)}, bf16[1792,128]{1,0:T(8,128)(2,1)}, bf16[1792,896]{1,0:T(8,128)(2,1)}, b...) custom-call(f32[233000,1,128]{2,1,0:T(1,128)} %get-tuple-element.40.flat), custom_call_target="tpu_custom_call" | custom-call | flops 200000000 | bytes 100000000 | tf_op jit(solution)/shard_map/unpack_early/pallas_call | solution.py:174
  961.0 1.3 reduce
  962.3 42.8 %new_state.1 = (f32[29125,128]{1,0:T(8,128)}, f32[29125,128]{1,0:T(8,128)}, f32[29125,128]{1,0:T(8,128)}) custom-call(f32[29125,1,128]{2,1,0:T(1,128)} %get-tuple-element.35.g, f32[29125,128]{1,0:T(8,128)} %bitcast.27, f32[29125,128]{1,0:T(8,128)} %bitcast.29, f32[29125,128]{1,0:T(8,128)} %bitcast.31, f32[8,128]{1,0:T(8,128)} %get-tuple-element.36.norm, ...), custom_call_target="tpu_custom_call" | custom-call | flops 200000000 | bytes 100000000 | tf_op jit(solution)/shard_map/new_state/pallas_call | solution.py:731
  1005.1 17.0 %all-gather.2.cloned.1.call-done.late = f32[43904,1,128]{2,1,0:T(1,128)} async-done(((f32[5488,1,128]{2,1,0:T(1,128)}), f32[43904,1,128]{2,1,0:T(1,128)}) %all-gather.2.cloned.1.call-update) | async-done | bytes 22478864 | tf_op jit(solution)/shard_map/all_gather | solution.py:752
  1022.1 12.9 %unpack_late.1 = (bf16[1792,896]{1,0:T(8,128)(2,1)}, bf16[1792,4864]{1,0:T(8,128)(2,1)}, bf16[1792,4864]{1,0:T(8,128)(2,1)}, bf16[9728,896]{1,0:T(8,128)(2,1)}) custom-call(f32[233000,1,128]{2,1,0:T(1,128)} %get-tuple-element.40.flat, ...), custom_call_target="tpu_custom_call", output_to_operand_aliasing={{0}: (2, {}), {1}: (3, {}), {2}: (4, {}), {3}: (5, {})} | custom-call | flops 200000000 | bytes 100000000 | tf_op jit(solution)/shard_map/unpack_late/pallas_call | solution.py:196
Async XLA Ops:
  7.2 1015.0 %all-gather.2.cloned.1.call-start = ((), (), s32[]{:S(2)}) async-start(), calls=%async_computation | async-start | bytes 25288704 | tf_op jit(solution)/shard_map/all_gather | solution.py:752
Sparse Core Ops, SparseCore 0:
  912.8 109.3 all-gather.1

commit v4 on v3

--- a/solution.py
+++ b/solution.py
@@ -1,4 +1,3 @@
-import functools
 import math
 import jax
 import jax.numpy as jnp
@@ -40,6 +39,7 @@
 GROUPS = {38: (16,), 7: (16, 32, 64), 1: (16, 128, 256)}
 STAGE_ROWS = max(br * WIDTHS[t] for t, br in enumerate(BLOCK_ROWS))
 
+
 def split(refs, counts):
     refs = list(refs)
     return [[refs.pop(0) for _ in range(n)] for n in counts]
@@ -65,9 +65,9 @@
     return max(g for g in GROUPS[width] if rows % g == 0)
 
 
-PIECE = 912
-PIECES = 32
-LATE_FIRST, LATE_END = 25, 31
+PIECE = 480
+PIECES = 61
+LATE_FIRST, LATE_END = 51, 60
 LATE_ROWS = PIECE * (LATE_END - LATE_FIRST) + 16
 PIECE_LAST = SEG - (PIECES - 1) * PIECE
 HALF = (PIECES - LATE_END + LATE_FIRST) // 2
@@ -253,7 +253,7 @@
     (grads, norms, (g_out, norm_out, flat, land_p, land_d, land_n, land_s),
      (mine, part, first, second, sums, g_buf, ss, ss_all), tiles, (stage, tail),
      (p_send, p_recv, i_send, i_recv, load_sem, g_sem, ss_send, ss_recv, in_sem, out_sem, tail_sem)) = split(refs, (7, 3, 7, 8, 3, 2, 11))
-    me, other, dev_x, dev_y, dev_d = neighbours()
+    me, other, dev_x, dev_y, _ = neighbours()
     core, x, y = lax.rem(me, 2), lax.rem(me // 2, 2), me // 4
     barrier = pltpu.get_barrier_semaphore()
     for d in range(1, NDEV):
@@ -491,9 +491,11 @@
     return p - lr * (decay_term + adam_dir), new_m, new_v
 
 
-UP_ROWS = 1824
-UP_LAST = SEG - 15 * UP_ROWS
-SUB = 152
+STATE_ROWS = 2 * PIECE
+STATE_COUNT = SEG // STATE_ROWS
+STATE_LAST = SEG - STATE_COUNT * STATE_ROWS
+STATE_SLOTS = 4
+SUB = 160
 
 
 def decay_rows(me, start, rows):
@@ -615,8 +617,8 @@
     def late_piece(j):
         return late_store(late_p.at[j], 8 + PIECE * j, j)
 
-    edges = [late_store(new_p.at[1, HALF - 2, pl.ds(PIECE - 8, 8)], 0, 6),
-             late_store(new_p.at[1, HALF - 1, pl.ds(0, 8)], LATE_ROWS - 8, 7)]
+    edges = [late_store(new_p.at[1, HALF - 2, pl.ds(PIECE - 8, 8)], 0, LATE_END - LATE_FIRST),
+             late_store(new_p.at[1, HALF - 1, pl.ds(0, 8)], LATE_ROWS - 8, LATE_END - LATE_FIRST + 1)]
     for copy in edges:
         copy.start()
 
@@ -682,60 +684,84 @@
         in_specs=[ANY] * 4 + [VMEM_SPEC, SMEM_SPEC],
         out_specs=[ANY, ANY],
         scratch_shapes=[buf, buf, buf, buf, pltpu.VMEM((2, HALF, PIECE, LANES), F32), pltpu.VMEM((LATE_END - LATE_FIRST, PIECE, LANES), F32),
-                        DMA((4, 2)), pairs, DMA((8,)), triples, triples, pairs, pairs, triples, triples],
+                        DMA((4, 2)), pairs, DMA((LATE_END - LATE_FIRST + 2,)), triples, triples, pairs, pairs, triples, triples],
         compiler_params=pltpu.CompilerParams(collective_id=1, has_side_effects=True, vmem_limit_bytes=VMEM_LIMIT),
         cost_estimate=COST,
     )(g, m, v, p, norm, lr)
 
 
-def state_kernel(g, m, v, p, norm, lr, new_p, new_m, new_v, gb, g_sem):
+def state_kernel(g, m, v, p, norm, lr, new_p, new_m, new_v, gb, mb, vb, pb, pn, mn, vn, in_sem, out_sem):
     me = lax.axis_index("dp")
-    i = pl.program_id(0)
-
-    def load(j, last):
-        rows = UP_LAST if last else UP_ROWS
-        return pltpu.make_async_copy(g.at[pl.ds(j * UP_ROWS, rows), 0], gb.at[lax.rem(j, 2), pl.ds(0, rows)], g_sem.at[lax.rem(j, 2)])
-
-    @pl.when(i == 0)
-    def _():
-        load(i, False).start()
-
-    @pl.when(i < 14)
-    def _():
-        load(i + 1, False).start()
-
-    @pl.when(i == 14)
-    def _():
-        load(i + 1, True).start()
-
-    @pl.when(i < 15)
-    def _():
-        load(i, False).wait()
-
-    @pl.when(i == 15)
-    def _():
-        load(i, True).wait()
-
-    norm_row = norm[0:1, :]
-
-    @pl.loop(0, UP_ROWS // SUB)
-    def _(s):
-        start = pl.multiple_of(s * SUB, 8)
-        rows = pl.ds(start, SUB)
-        new_p[rows], new_m[rows], new_v[rows] = adam_rows(
-            gb[lax.rem(i, 2), rows], m[rows], v[rows], p[rows], norm_row, lr[0], decay_rows(me, i * UP_ROWS + start, SUB))
+    norm_row = norm[pl.ds(0, 1), :]
+
+    def window(i):
+        rows = STATE_LAST if isinstance(i, int) and i == STATE_COUNT else STATE_ROWS
+        slot = lax.rem(i, STATE_SLOTS)
+        return slot, pl.ds(pl.multiple_of(i * STATE_ROWS, 8), rows), pl.ds(0, rows)
+
+    def loads(i):
+        slot, rows, size = window(i)
+        pairs = ((g.at[rows, 0], gb), (m.at[rows], mb), (v.at[rows], vb), (p.at[rows], pb))
+        return [pltpu.make_async_copy(src, buf.at[slot, size], in_sem.at[n, slot]) for n, (src, buf) in enumerate(pairs)]
+
+    def stores(i):
+        slot, rows, size = window(i)
+        pairs = ((pn, new_p), (mn, new_m), (vn, new_v))
+        return [pltpu.make_async_copy(buf.at[slot, size], dst.at[rows], out_sem.at[n, slot]) for n, (buf, dst) in enumerate(pairs)]
+
+    def run(copies, wait=False):
+        for copy in copies:
+            copy.wait() if wait else copy.start()
+
+    def compute(i):
+        slot = lax.rem(i, STATE_SLOTS)
+
+        @pl.loop(0, STATE_ROWS // SUB)
+        def _(s):
+            start = pl.multiple_of(s * SUB, 8)
+            rows = pl.ds(start, SUB)
+            pn[slot, rows], mn[slot, rows], vn[slot, rows] = adam_rows(
+                gb[slot, rows], mb[slot, rows], vb[slot, rows], pb[slot, rows], norm_row, lr[0],
+                decay_rows(me, i * STATE_ROWS + start, SUB))
+
+    for i in range(STATE_SLOTS):
+        run(loads(i))
+
+    @pl.loop(0, STATE_COUNT)
+    def _(i):
+        run(loads(i), wait=True)
+
+        @pl.when(i >= STATE_SLOTS)
+        def _():
+            run(stores(i - STATE_SLOTS), wait=True)
+
+        compute(i)
+        run(stores(i))
+
+        @pl.when(i + STATE_SLOTS < STATE_COUNT)
+        def _():
+            run(loads(i + STATE_SLOTS))
+
+        @pl.when(i + STATE_SLOTS == STATE_COUNT)
+        def _():
+            run(loads(STATE_COUNT))
+
+    run(loads(STATE_COUNT), wait=True)
+    run(stores(STATE_COUNT - STATE_SLOTS), wait=True)
+    compute(STATE_COUNT)
+    run(stores(STATE_COUNT))
+    for n in range(STATE_SLOTS):
+        run(stores(STATE_COUNT - STATE_SLOTS + 1 + n), wait=True)
 
 
 def new_state(g, m, v, p, norm, lr):
-    block = pl.BlockSpec((UP_ROWS, LANES), lambda i: (i, 0))
     return pl.pallas_call(
         state_kernel,
         name="new_state",
-        grid=(16,),
         out_shape=[jax.ShapeDtypeStruct((SEG, LANES), F32)] * 3,
-        in_specs=[ANY, block, block, block, pl.BlockSpec((8, LANES), lambda i: (0, 0)), SMEM_SPEC],
-        out_specs=[block] * 3,
-        scratch_shapes=[pltpu.VMEM((2, UP_ROWS, LANES), F32), DMA((2,))],
+        in_specs=[ANY] * 4 + [VMEM_SPEC, SMEM_SPEC],
+        out_specs=[ANY] * 3,
+        scratch_shapes=[pltpu.VMEM((STATE_SLOTS, STATE_ROWS, LANES), F32)] * 7 + [DMA((4, STATE_SLOTS)), DMA((3, STATE_SLOTS))],
         compiler_params=pltpu.CompilerParams(vmem_limit_bytes=VMEM_LIMIT),
         cost_estimate=COST,
     )(g, m, v, p, norm, lr)

time: 1050 us -> 1050 us (level)
  Pallas kernels: 1010 us -> 1030 us
  waiting for transfers between devices: 17 us -> 0.04 us
    pallas_call x1, Pallas kernels: 399 us -> 422 us  [gather_params(): pl.pallas_call(gather_kernel, name='gather_params', out_shape=[jax.ShapeD...]
    all_gather x1, waiting for transfers between devices: 17 us -> 0.02 us  [local_step(): late = lax.all_gather(late, 'dp', tiled=True)]
  transfers between devices with their start and end apart: 1 -> 1, of which waited for: 1 -> 0; matrix products, arithmetic and copies ran while one was open for 0% -> 0% of each run, Pallas kernels for 9% -> 8%
where the time goes in v4:
time: 1050 us; the launch traced here: 1040 us
  Pallas kernels  1030 us (98%)
  between operations  14.7 us (1%)
    pallas_call x1, Pallas kernels, reduce_grads(): pl.pallas_call(reduce_kernel, name='reduce_grads', out_shape=[jax.ShapeDt...  506 us
    pallas_call x1, Pallas kernels, gather_params(): pl.pallas_call(gather_kernel, name='gather_params', out_shape=[jax.ShapeD...  422 us
    pallas_call x1, Pallas kernels, unpack_early(): pl.pallas_call(unpack_early_kernel, name='unpack_early', out_shape=TENSOR...  52.5 us
    pallas_call x1, Pallas kernels, new_state(): pl.pallas_call(state_kernel, name='new_state', out_shape=[jax.ShapeDtypeS...  35.8 us
  transfers between devices with their start and end apart: 1, of which 0 were waited for; matrix products, arithmetic and copies ran while one was open for 0% of the time, Pallas kernels for 8%

profile of v4, /device:TPU:0, one launch (start us, length us, event | category | flops | bytes accessed | tf_op | source)
XLA Modules:
  0.0 1044.1 jit_solution(10387862833233774120)
XLA Ops:
  7.2 0.0 all-gather.2.cloned.1.call-start
  7.9 505.9 %reduce_grads.1 = (f32[29125,1,128]{2,1,0:T(1,128)}, f32[8,128]{1,0:T(8,128)}, f32[4,4,2,2,4860,1,128]{6,5,4,3,2,1,0:T(1,128)}, f32[4,2,16,911,1,128]{5,4,3,2,1,...) custom-call(bf16[1792,896]{1,0:T(8,128)(2,1)} %bitcast.38, ...), custom_call_target="tpu_custom_call" | custom-call | flops 200000000 | bytes 100000000 | tf_op jit(solution)/shard_map/reduce_grads/pallas_call | solution.py:469
  513.8 421.8 %gather_params.1 = (f32[233000,1,128]{2,1,0:T(1,128)}, f32[4336,1,128]{2,1,0:T(1,128)}) custom-call(f32[29125,1,128]{2,1,0:T(1,128)} %get-tuple-element.35.g, f32[29125,128]{1,0:T(8,128)} %bitcast.26, f32[29125,128]{1,0:T(8,128)} %bitcast.28, f32[29125,128]{1,0:T(8,128)} %bitcast.30, f32[8,128]{1,0:T(8,128)} %get-tuple-element.36.norm, f32[1]{0:T(128)} %bitcast.25.lr), custom_call_target="tpu_custom_call" | custom-call | flops 200000000 | bytes 100000000 | tf_op jit(solution)/shard_map/gather_params/pallas_call | solution.py:680
  935.6 0.0 all-gather.2.cloned.1.call-update
  935.6 1.2 slice.3
  936.8 52.5 %unpack_early.1 = (bf16[1792,896]{1,0:T(8,128)(2,1)}, bf16[1792,128]{1,0:T(8,128)(2,1)}, bf16[1792,128]{1,0:T(8,128)(2,1)}, bf16[1792,896]{1,0:T(8,128)(2,1)}, b...) custom-call(f32[233000,1,128]{2,1,0:T(1,128)} %get-tuple-element.40.flat), custom_call_target="tpu_custom_call" | custom-call | flops 200000000 | bytes 100000000 | tf_op jit(solution)/shard_map/unpack_early/pallas_call | solution.py:174
  989.3 1.3 reduce
  990.6 35.8 %new_state.1 = (f32[29125,128]{1,0:T(8,128)}, f32[29125,128]{1,0:T(8,128)}, f32[29125,128]{1,0:T(8,128)}) custom-call(f32[29125,1,128]{2,1,0:T(1,128)} %get-tuple-element.35.g, f32[29125,128]{1,0:T(8,128)} %bitcast.27, f32[29125,128]{1,0:T(8,128)} %bitcast.29, f32[29125,128]{1,0:T(8,128)} %bitcast.31, f32[8,128]{1,0:T(8,128)} %get-tuple-element.36.norm, ...), custom_call_target="tpu_custom_call" | custom-call | flops 200000000 | bytes 100000000 | tf_op jit(solution)/shard_map/new_state/pallas_call | solution.py:758
  1026.4 0.0 all-gather.2.cloned.1.call-done.late
  1026.4 10.8 %unpack_late.1 = (bf16[1792,896]{1,0:T(8,128)(2,1)}, bf16[1792,4864]{1,0:T(8,128)(2,1)}, bf16[1792,4864]{1,0:T(8,128)(2,1)}, bf16[9728,896]{1,0:T(8,128)(2,1)}) custom-call(f32[233000,1,128]{2,1,0:T(1,128)} %get-tuple-element.40.flat, ...), custom_call_target="tpu_custom_call", output_to_operand_aliasing={{0}: (2, {}), {1}: (3, {}), {2}: (4, {}), {3}: (5, {})} | custom-call | flops 200000000 | bytes 100000000 | tf_op jit(solution)/shard_map/unpack_late/pallas_call | solution.py:196
Async XLA Ops:
  7.2 1019.2 %all-gather.2.cloned.1.call-start = ((), (), s32[]{:S(2)}) async-start(), calls=%async_computation | async-start | bytes 19980288 | tf_op jit(solution)/shard_map/all_gather | solution.py:778
Sparse Core Ops, SparseCore 0:
  935.8 89.2 all-gather.1
